TPU v7x, 256 devices: a whole 4x4x8 slice. The times are simulated.
256 devices in a mesh: dp: 16 (over z, core), seq: 16 (over x, y).
Axes of the slice: x: 4, y: 4, z: 8, core: 2. Of those that a mesh axis runs over, the one named last changes fastest.
Arguments:
- tokens: bfloat16 [256, 256, 1024], P(('dp', 'seq')), may hold values from -6 to 6
- queries: bfloat16 [256, 256, 1024], P(('dp', 'seq')), may hold values from -240 to 240
- keys: bfloat16 [256, 256, 1024], P(('dp', 'seq')), may hold values from -7 to 7
- values: bfloat16 [256, 256, 1024], P(('dp', 'seq')), may hold values from -6 to 6
- ln_gain: bfloat16 [1024], replicated, may hold values from 0.5 to 1.5
- mean_in: bfloat16 [1024, 2048], P(None, 'seq'), may hold values from -0.1875 to 0.1875
- sigma_in: bfloat16 [1024, 2048], P(None, 'seq'), may hold values from 0.0039978027 to 0.029907227
- noise_in: bfloat16 [1024, 2048], P(None, 'seq'), may hold values from -4 to 4
- mean_out: bfloat16 [2048, 1024], P('seq'), may hold values from -0.125 to 0.125
- sigma_out: bfloat16 [2048, 1024], P('seq'), may hold values from 0.0019989014 to 0.014953613
- noise_out: bfloat16 [2048, 1024], P('seq'), may hold values from -4 to 4
- flip_in: int32 [256, 1024], P('dp'), may hold values from -1 to 1, as said below
- flip_mid: int32 [256, 2048], P('dp', 'seq'), may hold values from -1 to 1, as said below
- flip_hidden: int32 [256, 2048], P('dp', 'seq'), may hold values from -1 to 1, as said below
- flip_out: int32 [256, 1024], P('dp'), may hold values from -1 to 1, as said below
- cotangent: bfloat16 [256, 256, 1024], P(('dp', 'seq')), may hold values from -0.75 to 0.75
Outputs:
- block_out: bfloat16 [256, 256, 1024], P(('dp', 'seq'))
- resid_grad: bfloat16 [256, 256, 1024], P(('dp', 'seq'))
- grad_mean_in: float32 [1024, 2048], P(None, 'seq')
- grad_sigma_in: float32 [1024, 2048], P(None, 'seq')
- grad_mean_out: float32 [2048, 1024], P('seq')
- grad_sigma_out: float32 [2048, 1024], P('seq')
Inputs may be any that keep to these rules, and one draw needn't show every extreme that they name: `flip_in`: each entry is -1 or +1. `flip_mid`: each entry is -1 or +1. `flip_hidden`: each entry is -1 or +1. `flip_out`: each entry is -1 or +1.
All inputs are finite; a program needn't handle non-finite values.
Results may differ from a plain program's by a relative error of at most 0.018.
Values may be sent and summed in bfloat16 or wider, within the bound.
A program may use at most 128 MiB of HBM per device.

v0:
```python
import jax
import jax.numpy as jnp
from jax import lax
from jax.sharding import Mesh
from jax.sharding import PartitionSpec as P

HEADS = 16
DP = ("dp_0", "dp_1")
DP_SEQ = ("dp_0", "dp_1", "seq")


def in_blocks(x, dim, count):
    shape = x.shape
    tiles = x.reshape(*shape[:dim], count, shape[dim] // count, *shape[dim + 1 :])
    return jnp.moveaxis(tiles, dim, 0)


def sum_at_owner(x, axis, dim):
    tiles = in_blocks(x, dim, lax.axis_size(axis))
    arrived = lax.all_to_all(tiles, axis, split_axis=0, concat_axis=0, tiled=True)
    return arrived.astype(jnp.float32).sum(axis=0)


def sum_in_two_steps(x, axes, dim):
    far, near = axes
    own = sum_at_owner(in_blocks(x, dim, lax.axis_size(far)), near, dim + 1)
    return jnp.sum(
        lax.all_to_all(own.astype(jnp.bfloat16), far, 0, 0, tiled=True).astype(jnp.float32), axis=0
    )


def rows_for(lines, count):
    spare = -lines.shape[0] % count
    if not spare:
        return lines
    return jnp.concatenate([lines, jnp.zeros((spare, *lines.shape[1:]), lines.dtype)])


def from_everyone(x, axis):
    copies = jnp.broadcast_to(x, (lax.axis_size(axis), *x.shape))
    return lax.all_to_all(copies, axis, split_axis=0, concat_axis=0, tiled=True)


def in_order(tiles, dim):
    shape = list(tiles.shape[1:])
    shape[dim] *= tiles.shape[0]
    return jnp.moveaxis(tiles, 0, dim).reshape(shape)


def gathered_by_axis(x, axes, dim):
    far, near = axes
    leading = from_everyone(x, far)
    tiles = jnp.swapaxes(from_everyone(leading, near), 0, 1)
    return in_order(tiles.reshape(-1, *x.shape), dim)


def total_of(x, axes):
    lines = x.reshape(-1, x.shape[-1])
    own = sum_in_two_steps(
        rows_for(lines, lax.axis_size(axes[0]) * lax.axis_size(axes[1])), axes, 0
    )
    whole = gathered_by_axis(own.astype(jnp.bfloat16), axes, 0)
    return whole[: len(lines)].reshape(x.shape).astype(jnp.float32)


def gelu_slope(pre):
    cdf = 0.5 * (1.0 + lax.erf(pre * 0.7071067811865476))
    pdf = jnp.exp(-0.5 * pre * pre) * 0.3989422804014327
    return cdf + pre * pdf


def contract_first(left, right):
    return lax.dot_general(
        left, right, (((0,), (0,)), ((), ())), preferred_element_type=jnp.float32
    )


def contract_last(left, right):
    return lax.dot_general(
        left, right, (((1,), (1,)), ((), ())), preferred_element_type=jnp.float32
    )


def body(
    tokens,
    queries,
    keys,
    values,
    ln_gain,
    mean_in,
    sigma_in,
    noise_in,
    mean_out,
    sigma_out,
    noise_out,
    flip_in,
    flip_mid,
    flip_hidden,
    flip_out,
    cotangent,
):
    bf = jnp.bfloat16
    f32 = jnp.float32
    own_images, patches, width = tokens.shape
    hidden_local = mean_in.shape[1]
    head_dim = width // HEADS
    scale = head_dim ** (-0.5)
    pert_in = (sigma_in.astype(f32) * noise_in.astype(f32)).astype(bf)
    pert_out = (sigma_out.astype(f32) * noise_out.astype(f32)).astype(bf)
    query_heads = queries.reshape(own_images, patches, HEADS, head_dim)
    key_heads = keys.reshape(own_images, patches, HEADS, head_dim)
    value_heads = values.reshape(own_images, patches, HEADS, head_dim)
    scores = (
        jnp.einsum("bqhe,bkhe->bhqk", query_heads, key_heads, preferred_element_type=f32) * scale
    )
    top = jnp.max(scores, axis=-1, keepdims=True)
    expd = jnp.exp(scores - top)
    total = jnp.sum(expd, axis=-1)
    accum = jnp.einsum("bhqk,bkhe->bqhe", expd.astype(bf), value_heads, preferred_element_type=f32)
    attn_out = (
        (accum / jnp.transpose(total, (0, 2, 1))[..., None])
        .reshape(own_images, patches, width)
        .astype(bf)
    )
    resid = (tokens.astype(f32) + attn_out.astype(f32)).astype(bf)
    resid_f = resid.astype(f32)
    centered = resid_f - jnp.mean(resid_f, axis=-1, keepdims=True)
    rstd = lax.rsqrt(jnp.mean(centered * centered, axis=-1, keepdims=True) + 1e-06)
    ahat = centered * rstd
    gain_f = ln_gain.astype(f32)
    normed = (ahat * gain_f).astype(bf)
    in_signs = flip_in.astype(bf)[:, None, :]
    in_signs_f = flip_in.astype(f32)[:, None, :]
    mid_signs = flip_mid.astype(bf)[:, None, :]
    mid_signs_f = flip_mid.astype(f32)[:, None, :]
    hid_signs = flip_hidden.astype(bf)[:, None, :]
    hid_signs_f = flip_hidden.astype(f32)[:, None, :]
    out_signs = flip_out.astype(bf)[:, None, :]
    out_signs_f = flip_out.astype(f32)[:, None, :]
    gathered = lax.all_gather(normed, "seq", axis=0, tiled=True)
    count = gathered.shape[0]
    signs = in_signs
    flat = gathered.reshape(-1, width)
    flat_flip = (gathered * signs).reshape(-1, width)
    plain = jnp.dot(flat, mean_in, preferred_element_type=f32).reshape(count, patches, hidden_local)
    noisy = jnp.dot(flat_flip, pert_in, preferred_element_type=f32).reshape(
        count, patches, hidden_local
    )
    pre = plain + noisy * mid_signs_f
    group_images = pre.shape[0]
    rows = group_images * patches
    hidden = jax.nn.gelu(pre, approximate=False).astype(bf)
    flipped_hidden = hidden * hid_signs
    count = lax.axis_size("seq") * own_images
    hb = hidden.reshape(-1, hidden_local)
    hfb = flipped_hidden.reshape(-1, hidden_local)
    plain = jnp.dot(hb, mean_out, preferred_element_type=f32).reshape(count, patches, width)
    noisy = jnp.dot(hfb, pert_out, preferred_element_type=f32).reshape(count, patches, width)
    mixed = lax.psum_scatter(
        (plain + noisy * out_signs_f).astype(jnp.bfloat16), "seq", scatter_dimension=0, tiled=True
    ).astype(jnp.float32)
    block_out = (resid_f + mixed).astype(bf)
    cot_all = lax.all_gather(cotangent, "seq", axis=0, tiled=True)
    cot_flat = cot_all.reshape(rows, width)
    cot_flip_flat = (cot_all * out_signs).reshape(rows, width)
    dhidden = contract_last(cot_flat, mean_out).reshape(group_images, patches, hidden_local)
    dhidden = (
        dhidden
        + contract_last(cot_flip_flat, pert_out).reshape(group_images, patches, hidden_local)
        * hid_signs_f
    )
    dpre = (dhidden * gelu_slope(pre)).astype(bf)
    dpre_flip = dpre * mid_signs
    local_mean_out = contract_first(hidden.reshape(rows, hidden_local), cot_flat)
    local_sigma_out = contract_first(
        flipped_hidden.reshape(rows, hidden_local), cot_flip_flat
    ) * noise_out.astype(f32)
    local_mean_in = contract_first(gathered.reshape(rows, width), dpre.reshape(rows, hidden_local))
    local_flip_in = contract_first(
        (gathered * in_signs).reshape(rows, width), dpre_flip.reshape(rows, hidden_local)
    )
    local_sigma_in = local_flip_in * noise_in.astype(f32)
    count = lax.axis_size("seq") * own_images
    drows = dpre.reshape(-1, hidden_local)
    dflip_rows = dpre_flip.reshape(-1, hidden_local)
    signs = in_signs_f
    plain = contract_last(drows, mean_in).reshape(count, patches, width)
    noisy = contract_last(dflip_rows, pert_in).reshape(count, patches, width)
    dnormed = lax.psum_scatter(
        (plain + noisy * signs).astype(jnp.bfloat16), "seq", scatter_dimension=0, tiled=True
    ).astype(jnp.float32)
    grad_mean_in, grad_sigma_in, grad_mean_out, grad_sigma_out = (
        total_of(local_mean_in.astype(jnp.bfloat16), ("dp_0", "dp_1")),
        total_of(local_sigma_in.astype(jnp.bfloat16), ("dp_0", "dp_1")),
        total_of(local_mean_out.astype(jnp.bfloat16), ("dp_0", "dp_1")),
        total_of(local_sigma_out.astype(jnp.bfloat16), ("dp_0", "dp_1")),
    )
    scaled = dnormed * gain_f
    back = rstd * (
        scaled
        - jnp.mean(scaled, axis=-1, keepdims=True)
        - ahat * jnp.mean(scaled * ahat, axis=-1, keepdims=True)
    )
    resid_grad = (cotangent.astype(f32) + back).astype(bf)
    return (block_out, resid_grad, grad_mean_in, grad_sigma_in, grad_mean_out, grad_sigma_out)


def solution(mesh):
    finer = Mesh(mesh.devices.reshape(8, 2, mesh.shape["seq"]), ("dp_0", "dp_1", "seq"))
    in_specs = (
        P(DP_SEQ, None, None),
        P(DP_SEQ, None, None),
        P(DP_SEQ, None, None),
        P(DP_SEQ, None, None),
        P(),
        P(None, "seq"),
        P(None, "seq"),
        P(None, "seq"),
        P("seq", None),
        P("seq", None),
        P("seq", None),
        P(DP, None),
        P(DP, "seq"),
        P(DP, "seq"),
        P(DP, None),
        P(DP_SEQ, None, None),
    )
    out_specs = (
        P(DP_SEQ, None, None),
        P(DP_SEQ, None, None),
        P(None, "seq"),
        P(None, "seq"),
        P("seq", None),
        P("seq", None),
    )
    return jax.shard_map(body, mesh=finer, in_specs=in_specs, out_specs=out_specs, check_vma=False)
```

profile of v0, /device:TPU:1, one launch (start us, length us, event | category | flops | bytes accessed | tf_op | source)
XLA Modules:
  0.0 400.2 jit_solution(12291250398245741434)
XLA Ops:
  8.7 1.2 copy.70
  9.9 1.2 copy.71
  12.9 0.9 divide_convert_fusion
  14.3 1.3 convert_reduce_fusion
  15.9 1.1 fusion.65
  17.7 72.2 %all-gather.5.cloned.1.call-done = bf16[16,256,1024]{2,1,0:T(8,128)(2,1)} async-done(((bf16[1,256,1024]{2,1,0:T(8,128)(2,1)}), bf16[16,256,1024]{2,1,0:T(8,128)(2,1)}) %all-gather.5.cloned.1.call-update) | async-done | bytes 8388624 | tf_op jit(solution)/shard_map/all_gather | solution.py:163
  89.9 7.0 %fusion.90 = f32[16,256,128]{2,1,0:T(8,128)} fusion(bf16[16,256,1024]{2,1,0:T(8,128)(2,1)} %all-gather.5.cloned.1.call-done, bf16[128,1024]{1,0:T(8,128)(2,1)S(1)} %copy-done.6), kind=kOutput, calls=%fused_computation.99 | convolution fusion | flops 1073741824 | bytes 10747904 | tf_op jit(solution)/shard_map/dot_general | solution.py:79
  96.9 71.5 %all-gather.3.cloned.1.call-done = bf16[16,256,1024]{2,1,0:T(8,128)(2,1)} async-done(((bf16[1,256,1024]{2,1,0:T(8,128)(2,1)}), bf16[16,256,1024]{2,1,0:T(8,128)(2,1)}) %all-gather.3.cloned.1.call-update) | async-done | bytes 8388624 | tf_op jit(solution)/shard_map/all_gather | solution.py:140
  168.5 6.0 %fusion.96 = f32[16,256,128]{2,1,0:T(8,128)S(1)} fusion(bf16[16,256,1024]{2,1,0:T(8,128)(2,1)} %all-gather.3.cloned.1.call-done, bf16[1024,128]{1,0:T(8,128)(2,1)S(1)} %copy-done), kind=kOutput, calls=%fused_computation.105 | convolution fusion | flops 1073741824 | bytes 10747904 | tf_op jit(solution)/shard_map/dot_general | solution.py:145
  174.6 3.3 fusion.75
  177.9 3.0 fusion.22
  180.9 8.1 %fusion.94 = f32[16,256,1024]{2,1,0:T(8,128)} fusion(bf16[16,256,128]{2,1,0:T(8,128)(2,1)S(1)} %fusion.22, bf16[1024,128]{1,0:T(8,128)(2,1)S(1)} %copy-done), kind=kOutput, calls=%fused_computation.103 | convolution fusion | flops 1073741824 | bytes 18087936 | tf_op jit(solution)/shard_map/dot_general | solution.py:79
  189.0 9.3 %add_convert_fusion = bf16[16,256,1024]{2,1,0:T(8,128)(2,1)} fusion(f32[16,256,1024]{2,1,0:T(8,128)} %fusion.94, f32[16,1024]{1,0:T(8,128)S(1)} %get-tuple-element.14, bf16[16,256,128]{2,1,0:T(8,128)(2,1)S(1)} %fusion.22, bf16[16,128]{1,0:T(8,128)(2,1)S(1)} %get-tuple-element.18, bf16[1024,128]{1,0:T(8,128)(2,1)S(1)} %copy-done.13, ...), kind=kOutput, calls=%fused_computation | convolution fusion | flops 1087373312 | bytes 26808320 | tf_op jit(solution)/shard_map/dot_general | solution.py:79
  199.2 6.0 %fusion.16 = bf16[16,256,128]{2,1,0:T(8,128)(2,1)S(1)} fusion(f32[16,256,128]{2,1,0:T(8,128)} %copy-done.4, u16[256,128]{1,0:T(8,128)(2,1)S(1)} %copy-done.15, u16[256,128]{1,0:T(8,128)(2,1)S(1)} %get-tuple-element.6), kind=kLoop, calls=%fused_computation.22 | loop fusion | flops 36700160 | bytes 3276800 | tf_op jit(solution)/shard_map/convert_element_type | solution.py:152
  205.2 8.3 %fusion.92 = f32[16,256,1024]{2,1,0:T(8,128)} fusion(bf16[16,256,128]{2,1,0:T(8,128)(2,1)S(1)} %fusion.16, bf16[128,1024]{1,0:T(8,128)(2,1)S(1)} %copy-done.6), kind=kOutput, calls=%fused_computation.101 | convolution fusion | flops 1073741824 | bytes 18087936 | tf_op jit(solution)/shard_map/dot_general | solution.py:157
  213.4 9.7 %add_convert_fusion.1 = bf16[16,256,1024]{2,1,0:T(8,128)(2,1)} fusion(f32[16,256,1024]{2,1,0:T(8,128)} %fusion.92, f32[16,1024]{1,0:T(8,128)S(1)} %get-tuple-element.17, bf16[16,256,128]{2,1,0:T(8,128)(2,1)S(1)} %fusion.16, bf16[16,128]{1,0:T(8,128)(2,1)S(1)} %copy-done.22, bf16[128,1024]{1,0:T(8,128)(2,1)S(1)} %copy-done.11, bf16[128,1024]{1,0:T(8,128)(2,1)S(1)} %copy-done.9), kind=kOutput, calls=%fused_computation.1 | convolution fusion | flops 1087373312 | bytes 26808320 | tf_op jit(solution)/shard_map/dot_general | solution.py:158
  223.2 5.0 %fusion.64 = bf16[128,1024]{1,0:T(8,128)(2,1)S(1)} fusion(bf16[16,256,128]{2,1,0:T(8,128)(2,1)S(1)} %fusion.16, bf16[16,256,1024]{2,1,0:T(8,128)(2,1)} %all-gather.5.cloned.1.call-done), kind=kOutput, calls=%fused_computation.69 | convolution fusion | flops 1073872896 | bytes 9699328 | tf_op jit(solution)/shard_map/dot_general | solution.py:73
  229.0 4.9 %fusion.60 = bf16[128,1024]{1,0:T(8,128)(2,1)S(1)} fusion(bf16[16,256,1024]{2,1,0:T(8,128)(2,1)} %all-gather.5.cloned.1.call-done, bf16[16,1024]{1,0:T(8,128)(2,1)S(1)} %copy-done.21, bf16[16,256,128]{2,1,0:T(8,128)(2,1)S(1)} %fusion.16, bf16[128,1024]{1,0:T(8,128)(2,1)S(1)} %copy-done.12, bf16[16,128]{1,0:T(8,128)(2,1)S(1)} %copy-done.22), kind=kOutput, calls=%fused_computation.67 | convolution fusion | flops 1078853632 | bytes 9998336 | tf_op jit(solution)/shard_map/dot_general | solution.py:73
  234.6 4.6 %all-to-all-start.12 = ((bf16[2,8,8,1024]{3,2,1,0:T(8,128)(2,1)}), bf16[2,8,8,1024]{3,2,1,0:T(8,128)(2,1)S(1)}, u32[]{:S(2)}, u32[]{:S(2)}) async-start(bf16[2,8,8,1024]{3,2,1,0:T(8,128)(2,1)} %bitcast.95), calls=%async_computation.12 | async-start | bytes 524288 | tf_op jit(solution)/shard_map/all_to_all | solution.py:20
  239.2 6.0 %fusion.63 = bf16[1024,128]{1,0:T(8,128)(2,1)S(1)} fusion(bf16[16,256,1024]{2,1,0:T(8,128)(2,1)} %all-gather.3.cloned.1.call-done, bf16[16,256,128]{2,1,0:T(8,128)(2,1)S(1)} %fusion.22), kind=kOutput, calls=%fused_computation.68 | convolution fusion | flops 1073872896 | bytes 9699328 | tf_op jit(solution)/shard_map/dot_general | solution.py:73
  245.2 6.1 %fusion.57 = bf16[1024,128]{1,0:T(8,128)(2,1)S(1)} fusion(bf16[16,256,1024]{2,1,0:T(8,128)(2,1)} %all-gather.3.cloned.1.call-done, bf16[16,1024]{1,0:T(8,128)(2,1)S(1)} %copy-done.19, bf16[16,256,128]{2,1,0:T(8,128)(2,1)S(1)} %fusion.22, bf16[1024,128]{1,0:T(8,128)(2,1)S(1)} %copy-done.14, bf16[16,128]{1,0:T(8,128)(2,1)S(1)} %get-tuple-element.18), kind=kOutput, calls=%fused_computation.66 | convolution fusion | flops 1078853632 | bytes 9998336 | tf_op jit(solution)/shard_map/dot_general | solution.py:73
  251.4 3.7 all-to-all-start.8
  256.2 3.9 all_to_all.80
  260.1 3.9 all_to_all.81
  264.1 6.7 %all-to-all-start.13 = ((bf16[8,8,1024]{2,1,0:T(8,128)(2,1)}), bf16[8,8,1024]{2,1,0:T(8,128)(2,1)S(1)}, u32[]{:S(2)}, u32[]{:S(2)}) async-start(bf16[8,8,1024]{2,1,0:T(8,128)(2,1)} %reduce_sum.155), calls=%async_computation.13 | async-start | bytes 262144 | tf_op jit(solution)/shard_map/all_to_all | solution.py:28
  271.5 7.2 %all-to-all-done.13 = bf16[8,8,1024]{2,1,0:T(8,128)(2,1)S(1)} async-done(((bf16[8,8,1024]{2,1,0:T(8,128)(2,1)}), bf16[8,8,1024]{2,1,0:T(8,128)(2,1)S(1)}, u32[]{:S(2)}, u32[]{:S(2)}) %all-to-all-start.13) | async-done | bytes 131104 | tf_op jit(solution)/shard_map/all_to_all | solution.py:28
  278.7 3.4 all-to-all-start.9
  282.8 7.2 %all-to-all-done.9 = bf16[8,8,1024]{2,1,0:T(8,128)(2,1)S(1)} async-done(((bf16[8,8,1024]{2,1,0:T(8,128)(2,1)}), bf16[8,8,1024]{2,1,0:T(8,128)(2,1)S(1)}, u32[]{:S(2)}, u32[]{:S(2)}) %all-to-all-start.9) | async-done | bytes 131104 | tf_op jit(solution)/shard_map/all_to_all | solution.py:28
  290.0 3.4 all-to-all-start.5
  294.1 7.2 %all-to-all-done.5 = bf16[8,64,128]{2,1,0:T(8,128)(2,1)S(1)} async-done(((bf16[8,64,128]{2,1,0:T(8,128)(2,1)}), bf16[8,64,128]{2,1,0:T(8,128)(2,1)S(1)}, u32[]{:S(2)}, u32[]{:S(2)}) %all-to-all-start.5) | async-done | bytes 131104 | tf_op jit(solution)/shard_map/all_to_all | solution.py:28
  301.3 3.4 all-to-all-start.1
  304.7 7.8 %all-to-all-done.1 = bf16[8,64,128]{2,1,0:T(8,128)(2,1)S(1)} async-done(((bf16[8,64,128]{2,1,0:T(8,128)(2,1)}), bf16[8,64,128]{2,1,0:T(8,128)(2,1)S(1)}, u32[]{:S(2)}, u32[]{:S(2)}) %all-to-all-start.1) | async-done | bytes 131104 | tf_op jit(solution)/shard_map/all_to_all | solution.py:28
  313.2 3.4 all-to-all-start.10
  316.6 7.8 %all-to-all-done.10 = bf16[8,8,1024]{2,1,0:T(8,128)(2,1)S(1)} async-done(((bf16[8,8,1024]{2,1,0:T(8,128)(2,1)}), bf16[8,8,1024]{2,1,0:T(8,128)(2,1)S(1)}, u32[]{:S(2)}, u32[]{:S(2)}) %all-to-all-start.10) | async-done | bytes 131104 | tf_op jit(solution)/shard_map/all_to_all | solution.py:41
  325.1 3.4 all-to-all-start.2
  328.6 7.8 %all-to-all-done.2 = bf16[8,64,128]{2,1,0:T(8,128)(2,1)S(1)} async-done(((bf16[8,64,128]{2,1,0:T(8,128)(2,1)}), bf16[8,64,128]{2,1,0:T(8,128)(2,1)S(1)}, u32[]{:S(2)}, u32[]{:S(2)}) %all-to-all-start.2) | async-done | bytes 131104 | tf_op jit(solution)/shard_map/all_to_all | solution.py:41
  336.4 11.3 %all_to_all.82 = bf16[2,8,64,128]{3,2,1,0:T(8,128)(2,1)S(1)} all-to-all(bf16[2,8,64,128]{3,2,1,0:T(8,128)(2,1)S(1)} %broadcast_in_dim.17), channel_id=1, replica_groups=mesh['dp_0'=8,'dp_1'=2,'seq'=16] {'dp_1'}, dimensions={0} | all-to-all | bytes 524288 | tf_op jit(solution)/shard_map/all_to_all | solution.py:41
  348.3 3.4 all-to-all-start.6
  351.7 0.8 copy_convert_fusion.3
  352.6 7.4 %all-to-all-done.6 = bf16[8,64,128]{2,1,0:T(8,128)(2,1)S(1)} async-done(((bf16[8,64,128]{2,1,0:T(8,128)(2,1)}), bf16[8,64,128]{2,1,0:T(8,128)(2,1)S(1)}, u32[]{:S(2)}, u32[]{:S(2)}) %all-to-all-start.6) | async-done | bytes 131104 | tf_op jit(solution)/shard_map/all_to_all | solution.py:41
  360.0 5.3 %all_to_all.83 = bf16[2,8,64,128]{3,2,1,0:T(8,128)(2,1)S(1)} all-to-all(bf16[2,8,64,128]{3,2,1,0:T(8,128)(2,1)S(1)} %broadcast_in_dim.19), channel_id=1, replica_groups=mesh['dp_0'=8,'dp_1'=2,'seq'=16] {'dp_1'}, dimensions={0} | all-to-all | bytes 524288 | tf_op jit(solution)/shard_map/all_to_all | solution.py:41
  365.9 3.4 all-to-all-start.14
  369.3 0.8 copy_convert_fusion.2
  370.2 7.3 %all-to-all-done.14 = bf16[8,8,1024]{2,1,0:T(8,128)(2,1)S(1)} async-done(((bf16[8,8,1024]{2,1,0:T(8,128)(2,1)}), bf16[8,8,1024]{2,1,0:T(8,128)(2,1)S(1)}, u32[]{:S(2)}, u32[]{:S(2)}) %all-to-all-start.14) | async-done | bytes 131104 | tf_op jit(solution)/shard_map/all_to_all | solution.py:41
  377.6 5.4 %all_to_all.84 = bf16[2,8,8,1024]{3,2,1,0:T(8,128)(2,1)S(1)} all-to-all(bf16[2,8,8,1024]{3,2,1,0:T(8,128)(2,1)S(1)} %broadcast_in_dim.21), channel_id=1, replica_groups=mesh['dp_0'=8,'dp_1'=2,'seq'=16] {'dp_1'}, dimensions={0} | all-to-all | bytes 524288 | tf_op jit(solution)/shard_map/all_to_all | solution.py:41
  383.7 3.8 all-to-all-start.15
  389.6 1.4 fusion.74
  391.0 2.6 fusion.70
  (106 shorter events, 16.0 us)
Async XLA Ops:
  7.2 161.3 %copy-start = (bf16[1024,128]{1,0:T(8,128)(2,1)S(1)}, bf16[1024,128]{1,0:T(8,128)(2,1)}, u32[]{:S(2)}) copy-start(bf16[1024,128]{1,0:T(8,128)(2,1)} %param.21) | copy-start | bytes 786436
  7.2 4.0 copy-start.7
  7.2 82.7 %all-gather.5.cloned.1.call-start = ((), (), s32[]{:S(2)}) async-start(), calls=%async_computation.19 | async-start | bytes 8912896 | tf_op jit(solution)/shard_map/all_gather | solution.py:163
  7.9 160.6 %all-gather.3.cloned.1.call-start = ((), (), s32[]{:S(2)}) async-start(), calls=%async_computation.18 | async-start | bytes 8912896 | tf_op jit(solution)/shard_map/all_gather | solution.py:140
  14.2 2.8 copy-start.23
  14.2 2.8 copy-start.24
  14.2 3.4 copy-start.16
  14.2 3.4 copy-start.17
  14.3 75.6 %copy-start.6 = (bf16[128,1024]{1,0:T(8,128)(2,1)S(1)}, bf16[128,1024]{1,0:T(8,128)(2,1)}, u32[]{:S(2)}) copy-start(bf16[128,1024]{1,0:T(8,128)(2,1)} %param.24) | copy-start | bytes 786436
  17.0 372.6 %reduce-scatter.9.cloned.1.call-start = ((), (), s32[]{:S(2)}) async-start(), calls=%async_computation.21 | async-start | bytes 8912896
  17.7 156.8 %copy-start.18 = (bf16[16,1024]{1,0:T(8,128)(2,1)}, bf16[16,1024]{1,0:T(8,128)(2,1)S(1)}, u32[]{:S(2)}) copy-start(bf16[16,1024]{1,0:T(8,128)(2,1)S(1)} %get-tuple-element.15) | copy-start | bytes 98308
  17.7 160.1 %copy-start.20 = (bf16[16,1024]{1,0:T(8,128)(2,1)}, bf16[16,1024]{1,0:T(8,128)(2,1)S(1)}, u32[]{:S(2)}) copy-start(bf16[16,1024]{1,0:T(8,128)(2,1)S(1)} %get-tuple-element.16) | copy-start | bytes 98308
  96.9 77.5 %copy-start.8 = (bf16[1024,128]{1,0:T(8,128)(2,1)S(1)}, bf16[1024,128]{1,0:T(8,128)(2,1)}, u32[]{:S(2)}) copy-start(bf16[1024,128]{1,0:T(8,128)(2,1)} %param.22) | copy-start | bytes 786436
  96.9 77.5 %copy-start.13 = (bf16[1024,128]{1,0:T(8,128)(2,1)S(1)}, bf16[1024,128]{1,0:T(8,128)(2,1)}, u32[]{:S(2)}) copy-start(bf16[1024,128]{1,0:T(8,128)(2,1)} %param.23) | copy-start | bytes 786436
  168.5 6.0 %copy-start.2 = (bf16[16,256,1024]{2,1,0:T(8,128)(2,1)S(1)}, bf16[16,256,1024]{2,1,0:T(8,128)(2,1)}, u32[]{:S(2)}) copy-start(bf16[16,256,1024]{2,1,0:T(8,128)(2,1)} %all-gather.3.cloned.1.call-done) | copy-start | bytes 25165828
  168.5 9.4 %slice-start = ((s8[8388608]{0:T(1024)(128)(4,1)}), s8[4194304]{0:T(1024)(128)(4,1)S(1)}, s32[]{:S(2)}) async-start(s8[8388608]{0:T(1024)(128)(4,1)} %bitcast.99), calls=%async_computation.22 | async-start | bytes 8388608
  174.5 3.4 slice-start.1
  174.5 3.4 copy-start.3
  174.5 3.4 copy-start.9
  174.5 3.4 copy-start.10
  174.5 3.4 copy-start.25
  177.9 3.1 copy-start.4
  198.3 0.8 copy-start.15
  198.3 192.7 %reduce-scatter.7.cloned.1.call-start = ((), (), s32[]{:S(2)}) async-start(), calls=%async_computation.20 | async-start | bytes 8912896
  205.1 8.3 %copy-start.11 = (bf16[128,1024]{1,0:T(8,128)(2,1)S(1)}, bf16[128,1024]{1,0:T(8,128)(2,1)}, u32[]{:S(2)}) copy-start(bf16[128,1024]{1,0:T(8,128)(2,1)} %param.26) | copy-start | bytes 786436
  205.1 8.3 %copy-start.22 = (bf16[16,128]{1,0:T(8,128)(2,1)S(1)}, bf16[16,128]{1,0:T(8,128)(2,1)}, u32[]{:S(2)}) copy-start(bf16[16,128]{1,0:T(8,128)(2,1)} %get-tuple-element.21) | copy-start | bytes 12292
  223.2 5.8 %copy-start.12 = (bf16[128,1024]{1,0:T(8,128)(2,1)S(1)}, bf16[128,1024]{1,0:T(8,128)(2,1)}, u32[]{:S(2)}) copy-start(bf16[128,1024]{1,0:T(8,128)(2,1)} %param.26) | copy-start | bytes 786436
  223.2 5.8 %copy-start.21 = (bf16[16,1024]{1,0:T(8,128)(2,1)S(1)}, bf16[16,1024]{1,0:T(8,128)(2,1)}, u32[]{:S(2)}) copy-start(bf16[16,1024]{1,0:T(8,128)(2,1)} %copy-done.20) | copy-start | bytes 98308
  234.6 16.8 %all-to-all-start.12 = ((bf16[2,8,8,1024]{3,2,1,0:T(8,128)(2,1)}), bf16[2,8,8,1024]{3,2,1,0:T(8,128)(2,1)S(1)}, u32[]{:S(2)}, u32[]{:S(2)}) async-start(bf16[2,8,8,1024]{3,2,1,0:T(8,128)(2,1)} %bitcast.95), calls=%async_computation.12 | async-start | bytes 524288 | tf_op jit(solution)/shard_map/all_to_all | solution.py:20
  239.2 6.0 %copy-start.14 = (bf16[1024,128]{1,0:T(8,128)(2,1)S(1)}, bf16[1024,128]{1,0:T(8,128)(2,1)}, u32[]{:S(2)}) copy-start(bf16[1024,128]{1,0:T(8,128)(2,1)} %param.23) | copy-start | bytes 786436
  239.2 6.0 %copy-start.19 = (bf16[16,1024]{1,0:T(8,128)(2,1)S(1)}, bf16[16,1024]{1,0:T(8,128)(2,1)}, u32[]{:S(2)}) copy-start(bf16[16,1024]{1,0:T(8,128)(2,1)} %copy-done.18) | copy-start | bytes 98308
  251.4 4.9 %all-to-all-start.8 = ((bf16[2,8,8,1024]{3,2,1,0:T(8,128)(2,1)}), bf16[2,8,8,1024]{3,2,1,0:T(8,128)(2,1)S(1)}, u32[]{:S(2)}, u32[]{:S(2)}) async-start(bf16[2,8,8,1024]{3,2,1,0:T(8,128)(2,1)} %bitcast.96), calls=%async_computation.8 | async-start | bytes 524288 | tf_op jit(solution)/shard_map/all_to_all | solution.py:20
  264.1 14.6 %all-to-all-start.13 = ((bf16[8,8,1024]{2,1,0:T(8,128)(2,1)}), bf16[8,8,1024]{2,1,0:T(8,128)(2,1)S(1)}, u32[]{:S(2)}, u32[]{:S(2)}) async-start(bf16[8,8,1024]{2,1,0:T(8,128)(2,1)} %reduce_sum.155), calls=%async_computation.13 | async-start | bytes 262144 | tf_op jit(solution)/shard_map/all_to_all | solution.py:28
  278.7 11.3 %all-to-all-start.9 = ((bf16[8,8,1024]{2,1,0:T(8,128)(2,1)}), bf16[8,8,1024]{2,1,0:T(8,128)(2,1)S(1)}, u32[]{:S(2)}, u32[]{:S(2)}) async-start(bf16[8,8,1024]{2,1,0:T(8,128)(2,1)} %reduce_sum.153), calls=%async_computation.9 | async-start | bytes 262144 | tf_op jit(solution)/shard_map/all_to_all | solution.py:28
  290.0 11.3 %all-to-all-start.5 = ((bf16[8,64,128]{2,1,0:T(8,128)(2,1)}), bf16[8,64,128]{2,1,0:T(8,128)(2,1)S(1)}, u32[]{:S(2)}, u32[]{:S(2)}) async-start(bf16[8,64,128]{2,1,0:T(8,128)(2,1)} %reduce_sum.151), calls=%async_computation.5 | async-start | bytes 262144 | tf_op jit(solution)/shard_map/all_to_all | solution.py:28
  301.3 11.2 %all-to-all-start.1 = ((bf16[8,64,128]{2,1,0:T(8,128)(2,1)}), bf16[8,64,128]{2,1,0:T(8,128)(2,1)S(1)}, u32[]{:S(2)}, u32[]{:S(2)}) async-start(bf16[8,64,128]{2,1,0:T(8,128)(2,1)} %reduce_sum.149), calls=%async_computation.1 | async-start | bytes 262144 | tf_op jit(solution)/shard_map/all_to_all | solution.py:28
  313.2 11.2 %all-to-all-start.10 = ((bf16[8,8,1024]{2,1,0:T(8,128)(2,1)}), bf16[8,8,1024]{2,1,0:T(8,128)(2,1)S(1)}, u32[]{:S(2)}, u32[]{:S(2)}) async-start(bf16[8,8,1024]{2,1,0:T(8,128)(2,1)} %broadcast_in_dim.20), calls=%async_computation.10 | async-start | bytes 262144 | tf_op jit(solution)/shard_map/all_to_all | solution.py:41
  325.1 11.2 %all-to-all-start.2 = ((bf16[8,64,128]{2,1,0:T(8,128)(2,1)}), bf16[8,64,128]{2,1,0:T(8,128)(2,1)S(1)}, u32[]{:S(2)}, u32[]{:S(2)}) async-start(bf16[8,64,128]{2,1,0:T(8,128)(2,1)} %broadcast_in_dim.16), calls=%async_computation.2 | async-start | bytes 262144 | tf_op jit(solution)/shard_map/all_to_all | solution.py:41
  348.3 11.6 %all-to-all-start.6 = ((bf16[8,64,128]{2,1,0:T(8,128)(2,1)}), bf16[8,64,128]{2,1,0:T(8,128)(2,1)S(1)}, u32[]{:S(2)}, u32[]{:S(2)}) async-start(bf16[8,64,128]{2,1,0:T(8,128)(2,1)} %broadcast_in_dim.18), calls=%async_computation.6 | async-start | bytes 262144 | tf_op jit(solution)/shard_map/all_to_all | solution.py:41
  365.9 11.6 %all-to-all-start.14 = ((bf16[8,8,1024]{2,1,0:T(8,128)(2,1)}), bf16[8,8,1024]{2,1,0:T(8,128)(2,1)S(1)}, u32[]{:S(2)}, u32[]{:S(2)}) async-start(bf16[8,8,1024]{2,1,0:T(8,128)(2,1)} %broadcast_in_dim.22), calls=%async_computation.14 | async-start | bytes 262144 | tf_op jit(solution)/shard_map/all_to_all | solution.py:41
  377.6 13.5 %copy-start.5 = (bf16[1,256,1024]{2,1,0:T(8,128)(2,1)S(1)}, bf16[1,256,1024]{2,1,0:T(8,128)(2,1)}, u32[]{:S(2)}) copy-start(bf16[1,256,1024]{2,1,0:T(8,128)(2,1)} %param.31) | copy-start | bytes 1572868
  383.7 5.0 %all-to-all-start.15 = ((bf16[2,8,8,1024]{3,2,1,0:T(8,128)(2,1)}), bf16[2,8,8,1024]{3,2,1,0:T(8,128)(2,1)S(1)}, u32[]{:S(2)}, u32[]{:S(2)}) async-start(bf16[2,8,8,1024]{3,2,1,0:T(8,128)(2,1)} %broadcast_in_dim.23), calls=%async_computation.15 | async-start | bytes 524288 | tf_op jit(solution)/shard_map/all_to_all | solution.py:41
  388.7 4.9 %copy-start.1 = (bf16[1024,128]{1,0:T(8,128)(2,1)S(1)}, bf16[1024,128]{1,0:T(8,128)(2,1)}, u32[]{:S(2)}) copy-start(bf16[1024,128]{1,0:T(8,128)(2,1)} %param.21) | copy-start | bytes 786436
Sparse Core Ops, SparseCore 0:
  10.4 79.4 all-gather.4
  92.9 75.5 all-gather.2
  198.5 89.4 reduce-scatter.8
  291.5 90.4 reduce-scatter.6
where the time goes:
time: 402 us; the launch traced here: 400 us
  waiting for transfers between devices  205 us (51%)
  matrix products  78.3 us (19%)
  starting transfers between devices  42.6 us (11%)
  blocking collectives  29.9 us (7%)
  other arithmetic  21.1 us (5%)
  between operations  14.3 us (4%)
  local copies, waits for them, and re-layouts  8.92 us (2%)
    all_gather x1, waiting for transfers between devices, body(): cot_all = lax.all_gather(cotangent, 'seq', axis=0, tiled=True)  72.2 us
    all_gather x1, waiting for transfers between devices, body(): gathered = lax.all_gather(normed, 'seq', axis=0, tiled=True)  71.5 us
    all_to_all x5, waiting for transfers between devices, from_everyone(): return lax.all_to_all(copies, axis, split_axis=0, concat_axis=0, tiled=True)  30.7 us
    all_to_all x4, waiting for transfers between devices, sum_in_two_steps(): lax.all_to_all(own.astype(jnp.bfloat16), far, 0, 0, tiled=True)  29.5 us
    dot_general x4, matrix products, contract_last(): lax.dot_general(left, right, (((1,), (1,)), ((), ())), preferred_element_...  27.4 us
    all_to_all x3, blocking collectives, from_everyone(): return lax.all_to_all(copies, axis, split_axis=0, concat_axis=0, tiled=True)  22 us
    dot_general x4, matrix products, contract_first(): lax.dot_general(left, right, (((0,), (0,)), ((), ())), preferred_element_...  21.9 us
    all_to_all x5, starting transfers between devices, from_everyone(): return lax.all_to_all(copies, axis, split_axis=0, concat_axis=0, tiled=True)  17.3 us
  transfers between devices with their start and end apart: 15, of which 12 were waited for; matrix products, arithmetic and copies ran while one was open for 19% of the time, Pallas kernels for 0%

commit v1 on v0

v1 whole, which is shorter than its diff:
```python
import functools

import jax
import jax.numpy as jnp
from jax import lax
from jax.experimental import pallas as pl
from jax.experimental.pallas import tpu as pltpu
from jax.sharding import Mesh
from jax.sharding import PartitionSpec as P

BF = jnp.bfloat16
F32 = jnp.float32
HEAD = 64
SIDE = 4
MESH_ID = pl.DeviceIdType.MESH
DP = ("z", "c")
SEQ = ("x", "y")
ALL = ("z", "c", "x", "y")


def dot_t(a, b):
    return lax.dot_general(a, b, (((1,), (1,)), ((), ())), preferred_element_type=F32)


def dot_0(a, b):
    return lax.dot_general(a, b, (((0,), (0,)), ((), ())), preferred_element_type=F32)


def dot_n(a, b):
    return jnp.dot(a, b, preferred_element_type=F32)


class Ring:
    def __init__(self, at, axis, block, sends, recvs, base):
        me = at[axis]
        self.me = me
        self.right = lax.rem(me + 1, SIDE)
        self.left = lax.rem(me + 3, SIDE)
        self.far = lax.rem(me + 2, SIDE)
        self.block = block
        self.sends, self.recvs, self.base = sends, recvs, base

        def device(pos):
            where = dict(at)
            where[axis] = pos
            return tuple(where[name] for name in ALL)

        self.to_right, self.to_left = device(self.right), device(self.left)
        self.live = {}

    def copy(self, slot, src, dst, right):
        return pltpu.make_async_remote_copy(
            src_ref=src,
            dst_ref=dst,
            send_sem=self.sends.at[self.base + slot],
            recv_sem=self.recvs.at[self.base + slot],
            device_id=self.to_right if right else self.to_left,
            device_id_type=MESH_ID,
        )

    def go(self, slot, src, dst, right):
        copy = self.copy(slot, src, dst, right)
        copy.start()
        self.live[slot] = copy

    def gather_start(self):
        for slot, half, right in ((0, 0, True), (1, 1, False), (2, 1, True), (3, 0, False)):
            ref = self.block(self.me, half)
            self.go(slot, ref, ref, right)

    def gather_forward(self):
        self.live[0].wait_recv()
        ref = self.block(self.left, 0)
        self.go(4, ref, ref, True)
        self.live[1].wait_recv()
        ref = self.block(self.right, 1)
        self.go(5, ref, ref, False)

    def gather_finish(self):
        for slot in (2, 3, 4, 5):
            self.live[slot].wait_recv()

    def scatter_start(self, near, once):
        self.near, self.once = near, once
        self.go(0, self.block(self.far, 0), near[0], True)
        self.go(1, self.block(self.far, 1), near[1], False)
        self.go(2, self.block(self.right, 1), once[1], True)
        self.go(3, self.block(self.left, 0), once[2], False)

    def scatter_forward(self, add):
        self.live[0].wait_recv()
        ref = self.block(self.right, 0)
        add(ref, self.near[0])
        self.go(4, ref, self.once[0], True)
        self.live[1].wait_recv()
        ref = self.block(self.left, 1)
        add(ref, self.near[1])
        self.go(5, ref, self.once[3], False)

    def scatter_finish(self, add):
        for slot in (2, 3, 4, 5):
            self.live[slot].wait_recv()
        add(self.block(self.me, 0), self.once[0], self.once[2])
        add(self.block(self.me, 1), self.once[1], self.once[3])

    def drain(self):
        for slot in sorted(self.live):
            self.live[slot].wait_send()


def add_into(ref, *others):
    if len(ref.shape) == 3:
        for i in range(ref.shape[0]):
            add_into(ref.at[i], *(other.at[i] for other in others))
        return
    total = ref[...].astype(F32)
    for other in others:
        total = total + other[...].astype(F32)
    ref[...] = total.astype(BF)


def kernel(
    nz,
    q_ref,
    k_ref,
    v_ref,
    tok_ref,
    cot_ref,
    gain_ref,
    io_ref,
    w_hbm,
    f_hbm,
    out_ref,
    grad_ref,
    sum_ref,
    w_all,
    f_all,
    f_peer,
    io_peer,
    rows,
    norm,
    norm_f,
    cot,
    cot_f,
    resid,
    hid,
    hid_f,
    slope,
    dpre,
    dpre_f,
    mine,
    theirs,
    arrived,
    part,
    near1,
    once1,
    near2,
    once2,
    zbuf,
    total,
    ag_s,
    ag_r,
    rs_s,
    rs_r,
    z_s,
    z_r,
    core_s,
    core_r,
    local,
):
    patches, width = tok_ref.shape
    share = w_hbm.shape[1]
    half = share // 2
    own_hidden = SIDE * SIDE * share
    band = SIDE * share
    nblk = min(256, width)
    at = {name: lax.axis_index(name) for name in ALL}
    z, c, x, y = (at[name] for name in ALL)
    s = x * SIDE + y
    partner = (z, 1 - c, x, y)

    barrier = pltpu.get_barrier_semaphore()
    greet = [
        partner,
        (z, c, lax.rem(x + 1, SIDE), y),
        (z, c, lax.rem(x + 3, SIDE), y),
        (z, c, x, lax.rem(y + 1, SIDE)),
        (z, c, x, lax.rem(y + 3, SIDE)),
    ] + [(lax.rem(z + d, nz), c, x, y) for d in range(1, nz)]
    for device in greet:
        pl.semaphore_signal(barrier, inc=1, device_id=device, device_id_type=MESH_ID)

    loads = [
        pltpu.make_async_copy(w_hbm.at[m], w_all.at[m, x, y], local.at[m]) for m in range(4)
    ] + [pltpu.make_async_copy(f_hbm, f_all.at[x, y], local.at[4])]
    for load in loads:
        load.start()
    for load in loads:
        load.wait()
    pl.semaphore_wait(barrier, len(greet))

    def to_partner(slot, src, dst):
        return pltpu.make_async_remote_copy(
            src_ref=src,
            dst_ref=dst,
            send_sem=core_s.at[slot],
            recv_sem=core_r.at[slot],
            device_id=partner,
            device_id_type=MESH_ID,
        )

    def halves(n):
        return lambda h: pl.ds(h * n, n)

    rows_of = halves(half)
    frows = halves(f_all.shape[2] // 2)

    def gather_rings(m, base):
        if m == 4:
            first = Ring(at, "x", lambda j, h: f_all.at[j, y, frows(h)], ag_s, ag_r, base)
            second = Ring(at, "y", lambda j, h: f_all.at[:, j, frows(h)], ag_s, ag_r, base + 6)
        elif m % 2 == 0:
            first = Ring(at, "x", lambda j, h: w_all.at[m, j, y, rows_of(h)], ag_s, ag_r, base)
            second = Ring(at, "y", lambda j, h: w_all.at[m, :, j, rows_of(h)], ag_s, ag_r, base + 6)
        else:
            first = Ring(at, "y", lambda j, h: w_all.at[m, x, j, rows_of(h)], ag_s, ag_r, base)
            second = Ring(at, "x", lambda j, h: w_all.at[m, j, :, rows_of(h)], ag_s, ag_r, base + 6)
        return first, second

    ag = [gather_rings(m, 12 * m) for m in range(5)]
    order = (4, 0, 1, 2, 3)
    send_cot = to_partner(0, cot_ref, cot.at[pl.ds(patches, patches)])
    send_io = to_partner(1, io_ref, io_peer)
    for m in (4, 0, 1):
        ag[m][0].gather_start()
    send_io.start()
    send_cot.start()
    for m in (2, 3):
        ag[m][0].gather_start()

    def attend(p):
        lanes = pl.ds(pl.multiple_of(p * 128, 128), 128)
        q2, k2, v2 = q_ref[:, lanes], k_ref[:, lanes], v_ref[:, lanes]
        outs = []
        for i in range(2):
            cols = slice(i * HEAD, (i + 1) * HEAD)
            scores = dot_t(q2[:, cols], k2[:, cols]) * (HEAD**-0.5)
            e = jnp.exp(scores - jnp.max(scores, axis=-1, keepdims=True))
            norm_by = jnp.sum(e, axis=-1, keepdims=True)
            outs.append(dot_n(e.astype(BF), v2[:, cols]) / norm_by)
        attn = jnp.concatenate(outs, axis=1).astype(BF)
        resid[:, lanes] = (tok_ref[:, lanes].astype(F32) + attn.astype(F32)).astype(BF)

    pairs = width // 128

    @pl.loop(0, pairs // 2)
    def _(p):
        attend(p)

    for m in order:
        ag[m][0].gather_forward()

    @pl.loop(pairs // 2, pairs)
    def _(p):
        attend(p)

    for m in (4, 0, 1):
        ag[m][0].gather_finish()
        ag[m][1].gather_start()

    chunk = min(64, patches)
    gain = gain_ref[...].astype(F32)

    def stats(r):
        xf = resid[r, :].astype(F32)
        centered = xf - jnp.mean(xf, axis=-1, keepdims=True)
        rstd = lax.rsqrt(jnp.mean(centered * centered, axis=-1, keepdims=True) + 1e-06)
        return xf, centered * rstd, rstd

    @pl.loop(0, patches // chunk)
    def _(i):
        r = pl.ds(pl.multiple_of(i * chunk, chunk), chunk)
        _, ahat, _ = stats(r)
        norm[r, :] = (ahat * gain).astype(BF)
        cot[r, :] = cot_ref[r, :]

    ag[4][1].gather_forward()
    for m in (2, 3):
        ag[m][0].gather_finish()
    ag[4][1].gather_finish()

    send_norm = to_partner(2, norm.at[pl.ds(0, patches)], norm.at[pl.ds(patches, patches)])
    send_norm.start()
    send_flip = to_partner(
        3, f_all.at[:, :, :, pl.ds(2 * share, 2 * share)], f_peer
    )
    send_flip.start()

    send_io.wait_recv()
    send_flip.wait_recv()
    def own_row(t):
        keep = lax.broadcasted_iota(jnp.int32, t.shape, 0) == s
        return jnp.sum(jnp.where(keep, t, 0.0), axis=0, keepdims=True)

    rows[0, 0:2, 0:width] = io_ref[0:2, :]
    rows[1, 0:2, 0:width] = io_peer[0:2, :]
    for i, table in ((0, f_all), (1, f_peer)):
        for a in range(SIDE):
            for b in range(0, SIDE, 2):
                one = own_row(table[a, b, :, 0 : 2 * share])
                two = own_row(table[a, b + 1, :, 0 : 2 * share])
                lanes = slice((a * SIDE + b) * share, (a * SIDE + b + 2) * share)
                rows[i, 2:3, lanes] = jnp.concatenate([one[:, :share], two[:, :share]], axis=1)
                rows[i, 3:4, lanes] = jnp.concatenate([one[:, share:], two[:, share:]], axis=1)

    send_cot.wait_recv()
    send_norm.wait_recv()

    @pl.loop(0, patches // chunk)
    def _(i):
        for image in range(2):
            r = pl.ds(pl.multiple_of(image * patches + i * chunk, chunk), chunk)
            norm_f[r, :] = norm[r, :] * rows[image, 0:1, 0:width].astype(BF)
            cot_f[r, :] = cot[r, :] * rows[image, 1:2, 0:width].astype(BF)

    for m in (0, 1):
        ag[m][1].gather_forward()
    for m in (2, 3):
        ag[m][1].gather_start()
    for m in (0, 1):
        ag[m][1].gather_finish()

    image_rows = [slice(i * patches, (i + 1) * patches) for i in range(2)]

    def weight(m, h):
        return w_all[m, h].reshape(band, width)

    def weight_grad(m, h, left, right):
        for n in range(width // nblk):
            cols = slice(n * nblk, (n + 1) * nblk)
            part[m, h, :, :, cols] = (
                dot_0(left, right[:, cols]).astype(BF).reshape(SIDE, share, nblk)
            )

    def forward(h):
        lanes = pl.ds(pl.multiple_of(h * band, band), band)
        for i, r in enumerate(image_rows):
            pre = dot_t(norm[r, :], weight(0, h))
            pre = pre + dot_t(norm_f[r, :], weight(1, h)) * rows[i, 2:3, lanes]
            cdf = 0.5 * (1.0 + lax.erf(pre * 0.7071067811865476))
            pdf = jnp.exp(-0.5 * pre * pre) * 0.3989422804014327
            slope[r, lanes] = cdf + pre * pdf
            unit = (pre * cdf).astype(BF)
            hid[r, lanes] = unit
            hid_f[r, lanes] = unit * rows[i, 3:4, lanes].astype(BF)
        weight_grad(2, h, hid[:, lanes], cot)
        weight_grad(3, h, hid_f[:, lanes], cot_f)

    def backward(h):
        lanes = pl.ds(pl.multiple_of(h * band, band), band)
        for i, r in enumerate(image_rows):
            dh = dot_t(cot[r, :], weight(2, h))
            dh = dh + dot_t(cot_f[r, :], weight(3, h)) * rows[i, 3:4, lanes]
            unit = (dh * slope[r, lanes]).astype(BF)
            dpre[r, lanes] = unit
            dpre_f[r, lanes] = unit * rows[i, 2:3, lanes].astype(BF)
        weight_grad(0, h, dpre[:, lanes], norm)
        weight_grad(1, h, dpre_f[:, lanes], norm_f)

    def scatter_rings(m, base):
        along_y = lambda j, h: part.at[m, :, j, rows_of(h)]
        along_x = lambda j, h: part.at[m, j, :, rows_of(h)]
        one = lambda j, h: part.at[m, j, y, rows_of(h)]
        two = lambda j, h: part.at[m, x, j, rows_of(h)]
        if m % 2 == 0:
            return Ring(at, "y", along_y, rs_s, rs_r, base), Ring(at, "x", one, rs_s, rs_r, base + 6)
        return Ring(at, "x", along_x, rs_s, rs_r, base), Ring(at, "y", two, rs_s, rs_r, base + 6)

    rs = [scatter_rings(m, 12 * m) for m in range(4)]

    def start1(m):
        rs[m][0].scatter_start([near1.at[m, k] for k in range(2)], [once1.at[m, k] for k in range(4)])

    def start2(m):
        rs[m][1].scatter_start([near2.at[m, k] for k in range(2)], [once2.at[m, k] for k in range(4)])

    row_groups = min(nz, 4)
    lane_groups = nz // row_groups
    zr, zl = share // row_groups, width // lane_groups

    def spot(j):
        return (
            pl.ds(pl.multiple_of(lax.div(j, lane_groups) * zr, zr), zr),
            pl.ds(pl.multiple_of(lax.rem(j, lane_groups) * zl, zl), zl),
        )

    z_live = {}

    def z_copy(m, d, stage, src, dst):
        copy = pltpu.make_async_remote_copy(
            src_ref=src,
            dst_ref=dst,
            send_sem=z_s.at[m, stage, d - 1],
            recv_sem=z_r.at[m, stage, d - 1],
            device_id=(lax.rem(z + d, nz), c, x, y),
            device_id_type=MESH_ID,
        )
        copy.start()
        z_live[m, stage, d] = copy

    def z_start(m):
        for d in range(1, nz):
            r, l = spot(lax.rem(z + d, nz))
            z_copy(m, d, 0, part.at[m, x, y, r, l], zbuf.at[m, d - 1])

    def z_spread(m):
        r, l = spot(z)
        acc = part[m, x, y, r, l].astype(F32)
        for d in range(1, nz):
            z_live[m, 0, d].wait_recv()
            acc = acc + zbuf[m, d - 1].astype(F32)
        total[m, c, r, l] = acc.astype(BF)
        for d in range(1, nz):
            place = total.at[m, c, r, l]
            z_copy(m, d, 1, place, place)

    z_last = {}

    def z_finish(m):
        for d in range(1, nz):
            z_live[m, 1, d].wait_recv()
        z_last[m] = to_partner(6 + m, total.at[m, c], total.at[m, c])
        z_last[m].start()

    bands = own_hidden // band

    @pl.loop(0, bands // 2)
    def _(h):
        forward(h)

    for m in (2, 3):
        ag[m][1].gather_forward()

    @pl.loop(bands // 2, bands)
    def _(h):
        forward(h)

    start1(2)
    start1(3)
    for m in (2, 3):
        ag[m][1].gather_finish()

    @pl.loop(0, bands // 2)
    def _(h):
        backward(h)

    for m in (2, 3):
        rs[m][0].scatter_forward(add_into)

    @pl.loop(bands // 2, bands)
    def _(h):
        backward(h)

    start1(0)
    start1(1)

    def project(left, left_f, m, sign):
        @pl.loop(0, width // nblk)
        def _(n):
            lanes = pl.ds(pl.multiple_of(n * nblk, nblk), nblk)
            plain = w_all[m, :, :, :, lanes].reshape(own_hidden, nblk)
            noisy = w_all[m + 1, :, :, :, lanes].reshape(own_hidden, nblk)
            for i, r in enumerate(image_rows):
                out = dot_n(left[r, :], plain)
                out = out + dot_n(left_f[r, :], noisy) * rows[i, sign : sign + 1, lanes]
                if i:
                    theirs[m // 2, :, lanes] = out.astype(BF)
                else:
                    mine[m // 2, :, lanes] = out

    project(hid, hid_f, 2, 1)
    send_mixed = to_partner(4, theirs.at[1], arrived.at[1])
    send_mixed.start()

    for m in (2, 3):
        rs[m][0].scatter_finish(add_into)
        start2(m)

    project(dpre, dpre_f, 0, 0)
    send_back = to_partner(5, theirs.at[0], arrived.at[0])
    send_back.start()

    for m in (2, 3):
        rs[m][1].scatter_forward(add_into)
    for m in (0, 1):
        rs[m][0].scatter_forward(add_into)

    send_mixed.wait_recv()
    send_back.wait_recv()

    @pl.loop(0, patches // chunk)
    def _(i):
        r = pl.ds(pl.multiple_of(i * chunk, chunk), chunk)
        xf, ahat, rstd = stats(r)
        out_ref[r, :] = (xf + mine[1, r, :] + arrived[1, r, :].astype(F32)).astype(BF)
        g = (mine[0, r, :] + arrived[0, r, :].astype(F32)) * gain
        back = rstd * (
            g
            - jnp.mean(g, axis=-1, keepdims=True)
            - ahat * jnp.mean(g * ahat, axis=-1, keepdims=True)
        )
        grad_ref[r, :] = (cot_ref[r, :].astype(F32) + back).astype(BF)

    for m in (2, 3):
        rs[m][1].scatter_finish(add_into)
        z_start(m)
    for m in (0, 1):
        rs[m][0].scatter_finish(add_into)
        start2(m)
    for m in (2, 3):
        z_spread(m)
    for m in (0, 1):
        rs[m][1].scatter_forward(add_into)
    for m in (2, 3):
        z_finish(m)
    for m in (0, 1):
        rs[m][1].scatter_finish(add_into)
        z_start(m)
    for m in (0, 1):
        z_spread(m)
    for m in (0, 1):
        z_finish(m)
    for m in (2, 3, 0, 1):
        z_last[m].wait_recv()
    sum_ref[...] = total[...]

    for first, second in ag + rs:
        first.drain()
        second.drain()
    for copy in z_live.values():
        copy.wait_send()
    for copy in [send_cot, send_io, send_norm, send_flip, send_mixed, send_back, *z_last.values()]:
        copy.wait_send()


def layer(q, k, v, tok, cot, gain, io, w, f, nz):
    patches, width = tok.shape
    share = w.shape[1]
    hidden = SIDE * SIDE * share
    both = 2 * patches
    row_groups = min(nz, 4)
    zr, zl = share // row_groups, width // (nz // row_groups)
    vmem = pl.BlockSpec(memory_space=pltpu.VMEM)
    any_space = pl.BlockSpec(memory_space=pl.ANY)
    dma = pltpu.SemaphoreType.DMA
    half = share // 2
    scratch = [
        pltpu.VMEM((4, SIDE, SIDE, share, width), BF),
        pltpu.VMEM((SIDE, SIDE, *f.shape), F32),
        pltpu.VMEM((SIDE, SIDE, f.shape[0], f.shape[1] // 2), F32),
        pltpu.VMEM(io.shape, F32),
        pltpu.VMEM((2, 8, max(width, hidden)), F32),
        pltpu.VMEM((both, width), BF),
        pltpu.VMEM((both, width), BF),
        pltpu.VMEM((both, width), BF),
        pltpu.VMEM((both, width), BF),
        pltpu.VMEM((patches, width), BF),
        pltpu.VMEM((both, hidden), BF),
        pltpu.VMEM((both, hidden), BF),
        pltpu.VMEM((both, hidden), F32),
        pltpu.VMEM((both, hidden), BF),
        pltpu.VMEM((both, hidden), BF),
        pltpu.VMEM((2, patches, width), F32),
        pltpu.VMEM((2, patches, width), BF),
        pltpu.VMEM((2, patches, width), BF),
        pltpu.VMEM((4, SIDE, SIDE, share, width), BF),
        pltpu.VMEM((4, 2, SIDE, half, width), BF),
        pltpu.VMEM((4, 4, SIDE, half, width), BF),
        pltpu.VMEM((4, 2, half, width), BF),
        pltpu.VMEM((4, 4, half, width), BF),
        pltpu.VMEM((4, nz - 1, zr, zl), BF),
        pltpu.VMEM((4, 2, share, width), BF),
        dma((60,)),
        dma((60,)),
        dma((48,)),
        dma((48,)),
        dma((4, 2, nz - 1)),
        dma((4, 2, nz - 1)),
        dma((10,)),
        dma((10,)),
        dma((5,)),
    ]
    return pl.pallas_call(
        functools.partial(kernel, nz),
        out_shape=(
            jax.ShapeDtypeStruct((patches, width), BF),
            jax.ShapeDtypeStruct((patches, width), BF),
            jax.ShapeDtypeStruct((4, 2, share, width), BF),
        ),
        in_specs=[vmem] * 7 + [any_space] * 2,
        out_specs=(vmem, vmem, vmem),
        scratch_shapes=scratch,
        compiler_params=pltpu.CompilerParams(
            collective_id=0, has_side_effects=True, vmem_limit_bytes=62 * 1024 * 1024
        ),
        name="layer",
    )(q, k, v, tok, cot, gain, io, w, f)


def body(
    tokens,
    queries,
    keys,
    values,
    ln_gain,
    mean_in,
    sigma_in,
    noise_in,
    mean_out,
    sigma_out,
    noise_out,
    flip_in,
    flip_mid,
    flip_hidden,
    flip_out,
    cotangent,
):
    nz = lax.axis_size("z")
    width = tokens.shape[-1]
    share = mean_in.shape[1] // 2
    c = lax.axis_index("c")
    s = lax.axis_index("x") * SIDE + lax.axis_index("y")
    pert_in = (sigma_in.astype(F32) * noise_in.astype(F32)).astype(BF)
    pert_out = (sigma_out.astype(F32) * noise_out.astype(F32)).astype(BF)

    def own(t, axis):
        return lax.dynamic_slice_in_dim(t, c * share, share, axis)

    w = jnp.stack([own(mean_in, 1).T, own(pert_in, 1).T, own(mean_out, 0), own(pert_out, 0)])
    mid, hidden = flip_mid.astype(F32), flip_hidden.astype(F32)
    pick = lambda t, first: jnp.where((c == 0) == first, t[:, :share], t[:, share:])
    f = jnp.concatenate(
        [pick(mid, True), pick(hidden, True), pick(mid, False), pick(hidden, False)], axis=1
    )
    io = jnp.stack(
        [lax.dynamic_index_in_dim(t, s, 0, False).astype(F32) for t in (flip_in, flip_out)]
    )
    io = jnp.pad(io, ((0, 6), (0, 0)))
    out, grad, sums = layer(
        queries[0], keys[0], values[0], tokens[0], cotangent[0], ln_gain.reshape(1, width), io, w, f, nz
    )
    sums = sums.astype(F32).reshape(4, 2 * share, width)
    grad_mean_in = sums[0].T
    grad_sigma_in = sums[1].T * noise_in.astype(F32)
    grad_mean_out = sums[2]
    grad_sigma_out = sums[3] * noise_out.astype(F32)
    return out[None], grad[None], grad_mean_in, grad_sigma_in, grad_mean_out, grad_sigma_out


def solution(mesh):
    finer = Mesh(mesh.devices.reshape(-1, 2, SIDE, SIDE), ALL)
    images = P(ALL, None, None)
    cols = P(None, SEQ)
    rows = P(SEQ, None)
    in_specs = (
        images,
        images,
        images,
        images,
        P(),
        cols,
        cols,
        cols,
        rows,
        rows,
        rows,
        P(DP, None),
        P(DP, SEQ),
        P(DP, SEQ),
        P(DP, None),
        images,
    )
    out_specs = (images, images, cols, cols, rows, rows)
    return jax.shard_map(body, mesh=finer, in_specs=in_specs, out_specs=out_specs, check_vma=False)
```

time: 402 us -> 148 us (0.37)
  waiting for transfers between devices: 205 us -> 0 us
  Pallas kernels: 0 us -> 131 us
  matrix products: 78.3 us -> 0 us
  starting transfers between devices: 42.6 us -> 0 us
  blocking collectives: 29.9 us -> 0 us
  other arithmetic: 21.1 us -> 4.1 us
  between operations: 14.3 us -> 0.82 us
    all_gather x2 -> x0, waiting for transfers between devices: 144 us -> none  [the longest x1 72.2 us: body(): cot_all = lax.all_gather(cotangent, 'seq', axis=0, tiled=True)]
    pallas_call x0 -> x1, Pallas kernels: none -> 131 us  [layer(): pl.pallas_call(functools.partial(kernel, nz), out_shape=(jax.ShapeDtypeSt...]
    dot_general x14 -> x0, matrix products: 78.3 us -> none  [the longest x4 27.4 us: contract_last(): lax.dot_general(left, right, (((1,), (1,)), ((), ())), preferred_element_...]
    all_to_all x11 -> x0, waiting for transfers between devices: 60.6 us -> none  [the longest x5 30.7 us: from_everyone(): return lax.all_to_all(copies, axis, split_axis=0, concat_axis=0, tiled=True)]
    all_to_all x11 -> x0, starting transfers between devices: 42.4 us -> none  [the longest x5 17.3 us: from_everyone(): return lax.all_to_all(copies, axis, split_axis=0, concat_axis=0, tiled=True)]
    all_to_all x5 -> x0, blocking collectives: 29.9 us -> none  [the longest x3 22 us: from_everyone(): return lax.all_to_all(copies, axis, split_axis=0, concat_axis=0, tiled=True)]
    convert_element_type x13 -> x5, other arithmetic: 14.5 us -> 0.87 us  [the longest x1 0.79 us: body(): lax.dynamic_index_in_dim(t, s, 0, False).astype(F32)]
    reduce_sum x12 -> x0, other arithmetic: 6.62 us -> none  [the longest x4 2.82 us: sum_at_owner(): return arrived.astype(jnp.float32).sum(axis=0)]
  transfers between devices with their start and end apart: 15 -> 0, of which waited for: 12 -> 0; matrix products, arithmetic and copies ran while one was open for 19% -> 0% of each run, Pallas kernels for 0% -> 0%
where the time goes in v1:
time: 148 us; the launch traced here: 147 us
  Pallas kernels  131 us (89%)
  local copies, waits for them, and re-layouts  11 us (7%)
  other arithmetic  4.1 us (3%)
    pallas_call x1, Pallas kernels, layer(): pl.pallas_call(functools.partial(kernel, nz), out_shape=(jax.ShapeDtypeSt...  131 us
    unnamed x28, local copies, waits for them, and re-layouts  6.95 us

profile of v1, /device:TPU:1, one launch (start us, length us, event | category | flops | bytes accessed | tf_op | source)
XLA Modules:
  0.0 147.1 jit_solution(9428359782252414339)
XLA Ops:
  0.6 0.0 copy-start
  0.7 0.0 copy-start.10
  0.7 0.0 copy-start.8
  0.7 0.0 copy-start.9
  0.7 0.0 copy-start.4
  0.7 0.7 copy-done.10
  1.4 0.6 reshape.24.gain_ref
  2.0 0.8 dynamic-slice_convert_fusion
  2.8 0.0 copy-done.8
  2.8 0.0 copy-done.9
  2.8 0.1 slice_select_fusion.1
  2.9 0.7 pad_maximum_fusion.1.f_hbm
  3.6 0.6 select_maximum_fusion.io_ref
  4.2 0.0 copy-done
  4.2 0.0 copy-done.4
  4.2 0.1 copy.24
  4.4 0.0 copy-start.1
  4.4 0.9 copy-done.1
  5.3 0.0 copy-start.7
  5.4 0.9 copy-done.7
  6.3 0.0 copy-start.5
  6.3 0.0 copy-start.6
  6.3 0.9 copy-done.5
  7.2 0.1 copy-done.6
  7.3 0.2 constant_dynamic-slice_fusion
  7.5 0.1 copy.28
  7.7 0.1 copy.27
  7.8 0.9 pad_maximum_fusion.w_hbm
  8.7 131.2 %layer.1 = (bf16[256,1024]{1,0:T(8,128)(2,1)}, bf16[256,1024]{1,0:T(8,128)(2,1)}, bf16[4,2,64,1024]{3,2,1,0:T(8,128)(2,1)}) custom-call(bf16[256,1024]{1,0:T(8,128)(2,1)} %bitcast.28, bf16[256,1024]{1,0:T(8,128)(2,1)} %bitcast.29, bf16[256,1024]{1,0:T(8,128)(2,1)} %bitcast.30, bf16[256,1024]{1,0:T(8,128)(2,1)} %bitcast.31, bf16[256,1024]{1,0:T(8,128)(2,1)} %bitcast.32, ...), custom_call_target="tpu_custom_call" | custom-call | tf_op jit(solution)/shard_map/layer/pallas_call | solution.py:593
  139.9 2.2 %fusion.4 = (f32[1,2,64,1024]{3,2,1,0:T(8,128)S(1)}, f32[1,2,64,1024]{3,2,1,0:T(8,128)}, f32[1,2,64,1024]{3,2,1,0:T(8,128)S(1)}, f32[1,2,64,1024]{3,2,1,0:T(8,128)S(1)}) fusion(bf16[4,2,64,1024]{3,2,1,0:T(8,128)(2,1)} %get-tuple-element.11), kind=kLoop, calls=%fused_computation.21 | loop fusion | bytes 4194304 | tf_op jit(solution)/shard_map/slice | solution.py:656
  142.1 0.9 bitcast_multiply_fusion.1
  143.0 0.1 bitcast_multiply_fusion
  143.0 1.0 copy.26
  144.0 0.0 copy-start.3
  144.0 1.0 copy.25
  145.0 0.0 copy-done.3
  145.1 0.0 copy-start.2
  145.1 0.8 copy.31
  145.9 0.4 copy-done.2
  146.3 0.8 copy.32
  (7 shorter events, 0.2 us)
Async XLA Ops:
  0.6 3.6 %copy-start = (bf16[128,1024]{1,0:T(8,128)(2,1)S(1)}, bf16[128,1024]{1,0:T(8,128)(2,1)}, u32[]{:S(2)}) copy-start(bf16[128,1024]{1,0:T(8,128)(2,1)} %param.24) | copy-start | bytes 786436
  0.7 0.7 copy-start.10
  0.7 2.1 %copy-start.8 = (s32[16,128]{1,0:T(8,128)S(1)}, s32[16,128]{1,0:T(8,128)}, u32[]{:S(2)}) copy-start(s32[16,128]{1,0:T(8,128)} %param.28) | copy-start | bytes 24580
  0.7 2.1 %copy-start.9 = (s32[16,128]{1,0:T(8,128)S(1)}, s32[16,128]{1,0:T(8,128)}, u32[]{:S(2)}) copy-start(s32[16,128]{1,0:T(8,128)} %param.29) | copy-start | bytes 24580
  0.7 3.5 %copy-start.4 = (bf16[1024,128]{1,0:T(8,128)(2,1)S(1)}, bf16[1024,128]{1,0:T(8,128)(2,1)}, u32[]{:S(2)}) copy-start(bf16[1024,128]{1,0:T(8,128)(2,1)} %param.23) | copy-start | bytes 786436
  4.4 1.0 copy-start.1
  5.3 0.9 copy-start.7
  6.3 0.9 copy-start.5
  6.3 1.0 copy-start.6
  144.0 1.0 copy-start.3
  145.1 1.2 copy-start.2

commit v2 on v1

--- a/solution.py
+++ b/solution.py
@@ -135,9 +135,8 @@
     sum_ref,
     w_all,
     f_all,
-    f_peer,
-    io_peer,
-    rows,
+    msg,
+    signs,
     norm,
     norm_f,
     cot,
@@ -172,16 +171,22 @@
     share = w_hbm.shape[1]
     half = share // 2
     own_hidden = SIDE * SIDE * share
-    band = SIDE * share
+    band = min(256, own_hidden)
+    per_band = band // (SIDE * share)
+    bands = own_hidden // band
     nblk = min(256, width)
+    nk = nz // 2
     at = {name: lax.axis_index(name) for name in ALL}
     z, c, x, y = (at[name] for name in ALL)
     s = x * SIDE + y
-    partner = (z, 1 - c, x, y)
+    zp, zk = lax.rem(z, 2), lax.div(z, 2)
+    other = z + 1 - 2 * zp
+    partner, mate, cross = (z, 1 - c, x, y), (other, c, x, y), (other, 1 - c, x, y)
 
     barrier = pltpu.get_barrier_semaphore()
     greet = [
         partner,
+        cross,
         (z, c, lax.rem(x + 1, SIDE), y),
         (z, c, lax.rem(x + 3, SIDE), y),
         (z, c, x, lax.rem(y + 1, SIDE)),
@@ -199,13 +204,13 @@
         load.wait()
     pl.semaphore_wait(barrier, len(greet))
 
-    def to_partner(slot, src, dst):
+    def remote(slot, src, dst, device):
         return pltpu.make_async_remote_copy(
             src_ref=src,
             dst_ref=dst,
             send_sem=core_s.at[slot],
             recv_sem=core_r.at[slot],
-            device_id=partner,
+            device_id=device,
             device_id_type=MESH_ID,
         )
 
@@ -227,14 +232,22 @@
             second = Ring(at, "x", lambda j, h: w_all.at[m, j, :, rows_of(h)], ag_s, ag_r, base + 6)
         return first, second
 
+    def slot_rows(i):
+        return pl.ds(i * patches, patches)
+
     ag = [gather_rings(m, 12 * m) for m in range(5)]
-    order = (4, 0, 1, 2, 3)
-    send_cot = to_partner(0, cot_ref, cot.at[pl.ds(patches, patches)])
-    send_io = to_partner(1, io_ref, io_peer)
+    sends = []
+
+    def send(slot, src, dst, device):
+        copy = remote(slot, src, dst, device)
+        copy.start()
+        sends.append(copy)
+        return copy
+
     for m in (4, 0, 1):
         ag[m][0].gather_start()
-    send_io.start()
-    send_cot.start()
+    cot_1 = send(0, cot_ref, cot.at[slot_rows(1)], partner)
+    cot_2 = send(1, cot_ref, cot.at[slot_rows(2)], mate)
     for m in (2, 3):
         ag[m][0].gather_start()
 
@@ -257,7 +270,7 @@
     def _(p):
         attend(p)
 
-    for m in order:
+    for m in (4, 0, 1, 2, 3):
         ag[m][0].gather_forward()
 
     @pl.loop(pairs // 2, pairs)
@@ -284,88 +297,103 @@
         norm[r, :] = (ahat * gain).astype(BF)
         cot[r, :] = cot_ref[r, :]
 
+    for m in (2, 3):
+        ag[m][0].gather_finish()
+        ag[m][1].gather_start()
+    norm_1 = send(3, norm.at[slot_rows(0)], norm.at[slot_rows(1)], partner)
+    norm_2 = send(4, norm.at[slot_rows(0)], norm.at[slot_rows(2)], mate)
     ag[4][1].gather_forward()
-    for m in (2, 3):
-        ag[m][0].gather_finish()
     ag[4][1].gather_finish()
 
-    send_norm = to_partner(2, norm.at[pl.ds(0, patches)], norm.at[pl.ds(patches, patches)])
-    send_norm.start()
-    send_flip = to_partner(
-        3, f_all.at[:, :, :, pl.ds(2 * share, 2 * share)], f_peer
-    )
-    send_flip.start()
-
-    send_io.wait_recv()
-    send_flip.wait_recv()
     def own_row(t):
         keep = lax.broadcasted_iota(jnp.int32, t.shape, 0) == s
         return jnp.sum(jnp.where(keep, t, 0.0), axis=0, keepdims=True)
 
-    rows[0, 0:2, 0:width] = io_ref[0:2, :]
-    rows[1, 0:2, 0:width] = io_peer[0:2, :]
-    for i, table in ((0, f_all), (1, f_peer)):
-        for a in range(SIDE):
-            for b in range(0, SIDE, 2):
-                one = own_row(table[a, b, :, 0 : 2 * share])
-                two = own_row(table[a, b + 1, :, 0 : 2 * share])
-                lanes = slice((a * SIDE + b) * share, (a * SIDE + b + 2) * share)
-                rows[i, 2:3, lanes] = jnp.concatenate([one[:, :share], two[:, :share]], axis=1)
-                rows[i, 3:4, lanes] = jnp.concatenate([one[:, share:], two[:, share:]], axis=1)
-
-    send_cot.wait_recv()
-    send_norm.wait_recv()
-
-    @pl.loop(0, patches // chunk)
-    def _(i):
-        for image in range(2):
-            r = pl.ds(pl.multiple_of(image * patches + i * chunk, chunk), chunk)
-            norm_f[r, :] = norm[r, :] * rows[image, 0:1, 0:width].astype(BF)
-            cot_f[r, :] = cot[r, :] * rows[image, 1:2, 0:width].astype(BF)
+    for t in range(4):
+        msg[t, 0:2, 0:width] = io_ref[0:2, :]
+    for a in range(SIDE):
+        picked = [own_row(f_all[a, b]) for b in range(SIDE)]
+        for t in range(4):
+            for kind in range(2):
+                lo = (kind * 4 + t) * share
+                first = kind * own_hidden + a * SIDE * share
+                msg[t, 2:3, first : first + SIDE * share] = jnp.concatenate(
+                    [row[:, lo : lo + share] for row in picked], axis=1
+                )
+    quarter = lambda core, parity: msg.at[2 * core + parity]
+    sign_1 = send(6, quarter(1 - c, zp), signs.at[1], partner)
+    sign_2 = send(7, quarter(c, 1 - zp), signs.at[2], mate)
+    sign_3 = send(8, quarter(1 - c, 1 - zp), signs.at[3], cross)
+    signs[0] = msg[2 * c + zp]
+
+    def flip(dst, src, slot, row):
+        @pl.loop(0, patches // chunk)
+        def _(i):
+            r = pl.ds(pl.multiple_of(slot * patches + i * chunk, chunk), chunk)
+            dst[r, :] = src[r, :] * signs[slot, row : row + 1, 0:width].astype(BF)
 
     for m in (0, 1):
         ag[m][1].gather_forward()
-    for m in (2, 3):
-        ag[m][1].gather_start()
+    flip(norm_f, norm, 0, 0)
+    flip(cot_f, cot, 0, 1)
+    for copy in (cot_1, norm_1, sign_1):
+        copy.wait_recv()
+    flip(norm_f, norm, 1, 0)
+    flip(cot_f, cot, 1, 1)
+    for m in (2, 3):
+        ag[m][1].gather_forward()
+    cot_2.wait_recv()
+    cot_3 = send(2, cot.at[slot_rows(2)], cot.at[slot_rows(3)], partner)
     for m in (0, 1):
         ag[m][1].gather_finish()
 
-    image_rows = [slice(i * patches, (i + 1) * patches) for i in range(2)]
-
     def weight(m, h):
-        return w_all[m, h].reshape(band, width)
-
-    def weight_grad(m, h, left, right):
-        for n in range(width // nblk):
-            cols = slice(n * nblk, (n + 1) * nblk)
-            part[m, h, :, :, cols] = (
-                dot_0(left, right[:, cols]).astype(BF).reshape(SIDE, share, nblk)
-            )
-
-    def forward(h):
-        lanes = pl.ds(pl.multiple_of(h * band, band), band)
-        for i, r in enumerate(image_rows):
+        return w_all[m, pl.ds(h * per_band, per_band)].reshape(band, width)
+
+    def spans(t):
+        i, h = lax.div(t, bands), lax.rem(t, bands)
+        return (
+            i,
+            h,
+            pl.ds(pl.multiple_of(i * patches, patches), patches),
+            pl.ds(pl.multiple_of(h * band, band), band),
+        )
+
+    def hidden_row(i, h):
+        return signs[i, 2:3, pl.ds(pl.multiple_of(own_hidden + h * band, band), band)]
+
+    def forward(first, last):
+        @pl.loop(first * bands, last * bands)
+        def _(t):
+            i, h, r, lanes = spans(t)
             pre = dot_t(norm[r, :], weight(0, h))
-            pre = pre + dot_t(norm_f[r, :], weight(1, h)) * rows[i, 2:3, lanes]
+            pre = pre + dot_t(norm_f[r, :], weight(1, h)) * signs[i, 2:3, lanes]
             cdf = 0.5 * (1.0 + lax.erf(pre * 0.7071067811865476))
             pdf = jnp.exp(-0.5 * pre * pre) * 0.3989422804014327
             slope[r, lanes] = cdf + pre * pdf
             unit = (pre * cdf).astype(BF)
             hid[r, lanes] = unit
-            hid_f[r, lanes] = unit * rows[i, 3:4, lanes].astype(BF)
-        weight_grad(2, h, hid[:, lanes], cot)
-        weight_grad(3, h, hid_f[:, lanes], cot_f)
-
-    def backward(h):
-        lanes = pl.ds(pl.multiple_of(h * band, band), band)
-        for i, r in enumerate(image_rows):
+            hid_f[r, lanes] = unit * hidden_row(i, h).astype(BF)
+
+    def backward(first, last):
+        @pl.loop(first * bands, last * bands)
+        def _(t):
+            i, h, r, lanes = spans(t)
             dh = dot_t(cot[r, :], weight(2, h))
-            dh = dh + dot_t(cot_f[r, :], weight(3, h)) * rows[i, 3:4, lanes]
+            dh = dh + dot_t(cot_f[r, :], weight(3, h)) * hidden_row(i, h)
             unit = (dh * slope[r, lanes]).astype(BF)
             dpre[r, lanes] = unit
-            dpre_f[r, lanes] = unit * rows[i, 2:3, lanes].astype(BF)
-        weight_grad(0, h, dpre[:, lanes], norm)
-        weight_grad(1, h, dpre_f[:, lanes], norm_f)
+            dpre_f[r, lanes] = unit * signs[i, 2:3, lanes].astype(BF)
+
+    def weight_grad(m, left, right):
+        @pl.loop(0, bands)
+        def _(h):
+            lhs = left[:, pl.ds(pl.multiple_of(h * band, band), band)]
+            for n in range(width // nblk):
+                cols = slice(n * nblk, (n + 1) * nblk)
+                part[m, pl.ds(h * per_band, per_band), :, :, cols] = (
+                    dot_0(lhs, right[:, cols]).astype(BF).reshape(per_band, SIDE, share, nblk)
+                )
 
     def scatter_rings(m, base):
         along_y = lambda j, h: part.at[m, :, j, rows_of(h)]
@@ -384,8 +412,8 @@
     def start2(m):
         rs[m][1].scatter_start([near2.at[m, k] for k in range(2)], [once2.at[m, k] for k in range(4)])
 
-    row_groups = min(nz, 4)
-    lane_groups = nz // row_groups
+    row_groups = min(nk, 2)
+    lane_groups = nk // row_groups
     zr, zl = share // row_groups, width // lane_groups
 
     def spot(j):
@@ -396,114 +424,147 @@
 
     z_live = {}
 
-    def z_copy(m, d, stage, src, dst):
+    def z_copy(m, stage, d, step, src, dst):
         copy = pltpu.make_async_remote_copy(
             src_ref=src,
             dst_ref=dst,
             send_sem=z_s.at[m, stage, d - 1],
             recv_sem=z_r.at[m, stage, d - 1],
-            device_id=(lax.rem(z + d, nz), c, x, y),
+            device_id=(lax.rem(z + step * d, nz), c, x, y),
             device_id_type=MESH_ID,
         )
         copy.start()
         z_live[m, stage, d] = copy
 
     def z_start(m):
-        for d in range(1, nz):
-            r, l = spot(lax.rem(z + d, nz))
-            z_copy(m, d, 0, part.at[m, x, y, r, l], zbuf.at[m, d - 1])
+        for d in range(1, nk):
+            r, l = spot(lax.rem(zk + d, nk))
+            z_copy(m, 0, d, 2, part.at[m, x, y, r, l], zbuf.at[m, d - 1])
 
     def z_spread(m):
-        r, l = spot(z)
+        r, l = spot(zk)
         acc = part[m, x, y, r, l].astype(F32)
-        for d in range(1, nz):
+        for d in range(1, nk):
             z_live[m, 0, d].wait_recv()
             acc = acc + zbuf[m, d - 1].astype(F32)
-        total[m, c, r, l] = acc.astype(BF)
+        total[m, c, zp, r, l] = acc.astype(BF)
         for d in range(1, nz):
-            place = total.at[m, c, r, l]
-            z_copy(m, d, 1, place, place)
+            place = total.at[m, c, zp, r, l]
+            z_copy(m, 1, d, 1, place, place)
 
     z_last = {}
 
     def z_finish(m):
         for d in range(1, nz):
             z_live[m, 1, d].wait_recv()
-        z_last[m] = to_partner(6 + m, total.at[m, c], total.at[m, c])
-        z_last[m].start()
-
-    bands = own_hidden // band
-
-    @pl.loop(0, bands // 2)
-    def _(h):
-        forward(h)
-
-    for m in (2, 3):
-        ag[m][1].gather_forward()
-
-    @pl.loop(bands // 2, bands)
-    def _(h):
-        forward(h)
-
-    start1(2)
-    start1(3)
-    for m in (2, 3):
-        ag[m][1].gather_finish()
-
-    @pl.loop(0, bands // 2)
-    def _(h):
-        backward(h)
-
-    for m in (2, 3):
-        rs[m][0].scatter_forward(add_into)
-
-    @pl.loop(bands // 2, bands)
-    def _(h):
-        backward(h)
-
-    start1(0)
-    start1(1)
-
-    def project(left, left_f, m, sign):
+        z_last[m] = send(15 + m, total.at[m, c], total.at[m, c], partner)
+
+    def project(left, left_f, t, sign):
+        m = 2 * t
+
         @pl.loop(0, width // nblk)
         def _(n):
             lanes = pl.ds(pl.multiple_of(n * nblk, nblk), nblk)
             plain = w_all[m, :, :, :, lanes].reshape(own_hidden, nblk)
             noisy = w_all[m + 1, :, :, :, lanes].reshape(own_hidden, nblk)
-            for i, r in enumerate(image_rows):
+            for i in range(4):
+                r = slice(i * patches, (i + 1) * patches)
                 out = dot_n(left[r, :], plain)
-                out = out + dot_n(left_f[r, :], noisy) * rows[i, sign : sign + 1, lanes]
+                out = out + dot_n(left_f[r, :], noisy) * signs[i, sign : sign + 1, lanes]
                 if i:
-                    theirs[m // 2, :, lanes] = out.astype(BF)
+                    theirs[t, i - 1, :, lanes] = out.astype(BF)
                 else:
-                    mine[m // 2, :, lanes] = out
-
-    project(hid, hid_f, 2, 1)
-    send_mixed = to_partner(4, theirs.at[1], arrived.at[1])
-    send_mixed.start()
-
+                    mine[t, :, lanes] = out
+
+        base = 12 - 3 * t
+        to_pair = send(base, theirs.at[t, 0], arrived.at[t, 0], partner)
+        to_far = send(base + 1, theirs.at[t, 2], arrived.at[t, 1], partner)
+        return to_pair, to_far
+
+    def relay(t, to_far):
+        to_far.wait_recv()
+
+        @pl.loop(0, patches // chunk)
+        def _(i):
+            r = pl.ds(pl.multiple_of(i * chunk, chunk), chunk)
+            both = theirs[t, 1, r, :].astype(F32) + arrived[t, 1, r, :].astype(F32)
+            theirs[t, 1, r, :] = both.astype(BF)
+
+        return send(14 - 3 * t, theirs.at[t, 1], arrived.at[t, 2], mate)
+
+    forward(0, 2)
+    sign_2.wait_recv()
+    flip(cot_f, cot, 2, 1)
+    norm_2.wait_recv()
+    norm_3 = send(5, norm.at[slot_rows(2)], norm.at[slot_rows(3)], partner)
+    flip(norm_f, norm, 2, 0)
+    forward(2, 3)
+    sign_3.wait_recv()
+    cot_3.wait_recv()
+    flip(cot_f, cot, 3, 1)
+    norm_3.wait_recv()
+    flip(norm_f, norm, 3, 0)
+    forward(3, 4)
+    weight_grad(2, hid, cot)
+    start1(2)
+    weight_grad(3, hid_f, cot_f)
+    start1(3)
+    for m in (2, 3):
+        ag[m][1].gather_finish()
+    mixed_1, mixed_far = project(hid, hid_f, 1, 1)
+    backward(0, 4)
+    mixed_2 = relay(1, mixed_far)
+    for m in (2, 3):
+        rs[m][0].scatter_forward(add_into)
+    weight_grad(0, dpre, norm)
+    start1(0)
+    weight_grad(1, dpre_f, norm_f)
+    start1(1)
     for m in (2, 3):
         rs[m][0].scatter_finish(add_into)
         start2(m)
-
-    project(dpre, dpre_f, 0, 0)
-    send_back = to_partner(5, theirs.at[0], arrived.at[0])
-    send_back.start()
-
+    back_1, back_far = project(dpre, dpre_f, 0, 0)
+    for m in (0, 1):
+        rs[m][0].scatter_forward(add_into)
+    back_2 = relay(0, back_far)
     for m in (2, 3):
         rs[m][1].scatter_forward(add_into)
     for m in (0, 1):
-        rs[m][0].scatter_forward(add_into)
-
-    send_mixed.wait_recv()
-    send_back.wait_recv()
+        rs[m][0].scatter_finish(add_into)
+        start2(m)
+    for m in (2, 3):
+        rs[m][1].scatter_finish(add_into)
+        z_start(m)
+    for m in (0, 1):
+        rs[m][1].scatter_forward(add_into)
+    for m in (2, 3):
+        z_spread(m)
+    mixed_1.wait_recv()
+    mixed_2.wait_recv()
+
+    def gathered(t, r):
+        return mine[t, r, :] + arrived[t, 0, r, :].astype(F32) + arrived[t, 2, r, :].astype(F32)
 
     @pl.loop(0, patches // chunk)
     def _(i):
         r = pl.ds(pl.multiple_of(i * chunk, chunk), chunk)
-        xf, ahat, rstd = stats(r)
-        out_ref[r, :] = (xf + mine[1, r, :] + arrived[1, r, :].astype(F32)).astype(BF)
-        g = (mine[0, r, :] + arrived[0, r, :].astype(F32)) * gain
+        out_ref[r, :] = (resid[r, :].astype(F32) + gathered(1, r)).astype(BF)
+
+    for m in (0, 1):
+        rs[m][1].scatter_finish(add_into)
+        z_start(m)
+    for m in (2, 3):
+        z_finish(m)
+    for m in (0, 1):
+        z_spread(m)
+    back_1.wait_recv()
+    back_2.wait_recv()
+
+    @pl.loop(0, patches // chunk)
+    def _(i):
+        r = pl.ds(pl.multiple_of(i * chunk, chunk), chunk)
+        _, ahat, rstd = stats(r)
+        g = gathered(0, r) * gain
         back = rstd * (
             g
             - jnp.mean(g, axis=-1, keepdims=True)
@@ -511,23 +572,6 @@
         )
         grad_ref[r, :] = (cot_ref[r, :].astype(F32) + back).astype(BF)
 
-    for m in (2, 3):
-        rs[m][1].scatter_finish(add_into)
-        z_start(m)
-    for m in (0, 1):
-        rs[m][0].scatter_finish(add_into)
-        start2(m)
-    for m in (2, 3):
-        z_spread(m)
-    for m in (0, 1):
-        rs[m][1].scatter_forward(add_into)
-    for m in (2, 3):
-        z_finish(m)
-    for m in (0, 1):
-        rs[m][1].scatter_finish(add_into)
-        z_start(m)
-    for m in (0, 1):
-        z_spread(m)
     for m in (0, 1):
         z_finish(m)
     for m in (2, 3, 0, 1):
@@ -537,57 +581,55 @@
     for first, second in ag + rs:
         first.drain()
         second.drain()
-    for copy in z_live.values():
-        copy.wait_send()
-    for copy in [send_cot, send_io, send_norm, send_flip, send_mixed, send_back, *z_last.values()]:
+    for copy in [*z_live.values(), *sends]:
         copy.wait_send()
 
 
 def layer(q, k, v, tok, cot, gain, io, w, f, nz):
     patches, width = tok.shape
     share = w.shape[1]
+    half = share // 2
     hidden = SIDE * SIDE * share
-    both = 2 * patches
-    row_groups = min(nz, 4)
-    zr, zl = share // row_groups, width // (nz // row_groups)
+    four = 4 * patches
+    nk = nz // 2
+    row_groups = min(nk, 2)
+    zr, zl = share // row_groups, width // (nk // row_groups)
     vmem = pl.BlockSpec(memory_space=pltpu.VMEM)
     any_space = pl.BlockSpec(memory_space=pl.ANY)
     dma = pltpu.SemaphoreType.DMA
-    half = share // 2
     scratch = [
         pltpu.VMEM((4, SIDE, SIDE, share, width), BF),
         pltpu.VMEM((SIDE, SIDE, *f.shape), F32),
-        pltpu.VMEM((SIDE, SIDE, f.shape[0], f.shape[1] // 2), F32),
-        pltpu.VMEM(io.shape, F32),
-        pltpu.VMEM((2, 8, max(width, hidden)), F32),
-        pltpu.VMEM((both, width), BF),
-        pltpu.VMEM((both, width), BF),
-        pltpu.VMEM((both, width), BF),
-        pltpu.VMEM((both, width), BF),
+        pltpu.VMEM((4, 8, max(width, 2 * hidden)), F32),
+        pltpu.VMEM((4, 8, max(width, 2 * hidden)), F32),
+        pltpu.VMEM((four, width), BF),
+        pltpu.VMEM((four, width), BF),
+        pltpu.VMEM((four, width), BF),
+        pltpu.VMEM((four, width), BF),
         pltpu.VMEM((patches, width), BF),
-        pltpu.VMEM((both, hidden), BF),
-        pltpu.VMEM((both, hidden), BF),
-        pltpu.VMEM((both, hidden), F32),
-        pltpu.VMEM((both, hidden), BF),
-        pltpu.VMEM((both, hidden), BF),
+        pltpu.VMEM((four, hidden), BF),
+        pltpu.VMEM((four, hidden), BF),
+        pltpu.VMEM((four, hidden), F32),
+        pltpu.VMEM((four, hidden), BF),
+        pltpu.VMEM((four, hidden), BF),
         pltpu.VMEM((2, patches, width), F32),
-        pltpu.VMEM((2, patches, width), BF),
-        pltpu.VMEM((2, patches, width), BF),
+        pltpu.VMEM((2, 3, patches, width), BF),
+        pltpu.VMEM((2, 3, patches, width), BF),
         pltpu.VMEM((4, SIDE, SIDE, share, width), BF),
         pltpu.VMEM((4, 2, SIDE, half, width), BF),
         pltpu.VMEM((4, 4, SIDE, half, width), BF),
         pltpu.VMEM((4, 2, half, width), BF),
         pltpu.VMEM((4, 4, half, width), BF),
-        pltpu.VMEM((4, nz - 1, zr, zl), BF),
-        pltpu.VMEM((4, 2, share, width), BF),
+        pltpu.VMEM((4, nk - 1, zr, zl), BF),
+        pltpu.VMEM((4, 2, 2, share, width), BF),
         dma((60,)),
         dma((60,)),
         dma((48,)),
         dma((48,)),
         dma((4, 2, nz - 1)),
         dma((4, 2, nz - 1)),
-        dma((10,)),
-        dma((10,)),
+        dma((19,)),
+        dma((19,)),
         dma((5,)),
     ]
     return pl.pallas_call(
@@ -595,7 +637,7 @@
         out_shape=(
             jax.ShapeDtypeStruct((patches, width), BF),
             jax.ShapeDtypeStruct((patches, width), BF),
-            jax.ShapeDtypeStruct((4, 2, share, width), BF),
+            jax.ShapeDtypeStruct((4, 2, 2, share, width), BF),
         ),
         in_specs=[vmem] * 7 + [any_space] * 2,
         out_specs=(vmem, vmem, vmem),
@@ -627,21 +669,17 @@
 ):
     nz = lax.axis_size("z")
     width = tokens.shape[-1]
-    share = mean_in.shape[1] // 2
-    c = lax.axis_index("c")
+    share = mean_in.shape[1] // 4
+    quarter = lax.axis_index("c") * 2 + lax.rem(lax.axis_index("z"), 2)
     s = lax.axis_index("x") * SIDE + lax.axis_index("y")
     pert_in = (sigma_in.astype(F32) * noise_in.astype(F32)).astype(BF)
     pert_out = (sigma_out.astype(F32) * noise_out.astype(F32)).astype(BF)
 
     def own(t, axis):
-        return lax.dynamic_slice_in_dim(t, c * share, share, axis)
+        return lax.dynamic_slice_in_dim(t, quarter * share, share, axis)
 
     w = jnp.stack([own(mean_in, 1).T, own(pert_in, 1).T, own(mean_out, 0), own(pert_out, 0)])
-    mid, hidden = flip_mid.astype(F32), flip_hidden.astype(F32)
-    pick = lambda t, first: jnp.where((c == 0) == first, t[:, :share], t[:, share:])
-    f = jnp.concatenate(
-        [pick(mid, True), pick(hidden, True), pick(mid, False), pick(hidden, False)], axis=1
-    )
+    f = jnp.concatenate([flip_mid, flip_hidden], axis=1).astype(F32)
     io = jnp.stack(
         [lax.dynamic_index_in_dim(t, s, 0, False).astype(F32) for t in (flip_in, flip_out)]
     )
@@ -649,7 +687,7 @@
     out, grad, sums = layer(
         queries[0], keys[0], values[0], tokens[0], cotangent[0], ln_gain.reshape(1, width), io, w, f, nz
     )
-    sums = sums.astype(F32).reshape(4, 2 * share, width)
+    sums = sums.astype(F32).reshape(4, 4 * share, width)
     grad_mean_in = sums[0].T
     grad_sigma_in = sums[1].T * noise_in.astype(F32)
     grad_mean_out = sums[2]

time: 148 us -> 123 us (0.83)
  Pallas kernels: 131 us -> 107 us
  local copies, waits for them, and re-layouts: 11 us -> 9.22 us
    pallas_call x1, Pallas kernels: 131 us -> 107 us  [layer(): pl.pallas_call(functools.partial(kernel, nz), out_shape=(jax.ShapeDtypeSt...]
    unnamed x28 -> x20, local copies, waits for them, and re-layouts: 6.95 us -> 4.45 us
where the time goes in v2:
time: 123 us
  Pallas kernels  107 us (87%)
  local copies, waits for them, and re-layouts  9.22 us (7%)
  other arithmetic  5.4 us (4%)
    pallas_call x1, Pallas kernels, layer(): pl.pallas_call(functools.partial(kernel, nz), out_shape=(jax.ShapeDtypeSt...  107 us
    unnamed x20, local copies, waits for them, and re-layouts  4.45 us

profile of v2, /device:TPU:1, one launch (start us, length us, event | category | flops | bytes accessed | tf_op | source)
XLA Modules:
  0.0 122.7 jit_solution(13988353353839696102)
XLA Ops:
  0.6 0.0 copy-start
  0.6 0.0 copy-start.4
  0.7 1.3 %reshape.24.gain_ref = bf16[1,1024]{1,0:T(2,128)(2,1)} reshape(bf16[1024]{0:T(1024)(128)(2,1)} %param.20) | data formatting | bytes 4096 | tf_op jit(solution)/shard_map/reshape | solution.py:688
  2.0 0.8 dynamic-slice_convert_fusion
  2.8 1.3 %add_convert_fusion.f_hbm = f32[16,256]{1,0:T(8,128)} fusion(s32[16,128]{1,0:T(8,128)} %param.29, s32[16,128]{1,0:T(8,128)} %param.28), kind=kLoop, calls=%fused_computation.12 | loop fusion | flops 8192 | bytes 32768 | tf_op jit(solution)/shard_map/convert_element_type | solution.py:682
  4.1 0.6 select_maximum_fusion.io_ref
  4.7 0.0 copy-done
  4.8 0.0 copy-done.4
  4.8 0.1 copy.24
  4.9 0.0 copy-start.1
  5.0 0.9 copy-done.1
  5.9 0.0 copy-start.6
  5.9 0.0 copy-start.5
  5.9 0.9 fusion.3
  6.8 0.0 copy-done.6
  6.9 0.1 copy-done.5
  6.9 0.2 constant_dynamic-slice_fusion
  7.2 0.1 copy.28
  7.3 0.1 copy.27
  7.4 0.7 pad_maximum_fusion.w_hbm
  8.2 107.4 %layer.1 = (bf16[256,1024]{1,0:T(8,128)(2,1)}, bf16[256,1024]{1,0:T(8,128)(2,1)}, bf16[4,2,2,32,1024]{4,3,2,1,0:T(8,128)(2,1)}) custom-call(bf16[256,1024]{1,0:T(8,128)(2,1)} %bitcast.31, bf16[256,1024]{1,0:T(8,128)(2,1)} %bitcast.32, bf16[256,1024]{1,0:T(8,128)(2,1)} %bitcast.33, bf16[256,1024]{1,0:T(8,128)(2,1)} %bitcast.34, bf16[256,1024]{1,0:T(8,128)(2,1)} %bitcast.35, ...), custom_call_target="tpu_custom_call" | custom-call | tf_op jit(solution)/shard_map/layer/pallas_call | solution.py:635
  115.5 2.2 %fusion.4 = (f32[1,2,2,32,1024]{4,3,2,1,0:T(8,128)S(1)}, f32[1,2,2,32,1024]{4,3,2,1,0:T(8,128)}, f32[1,2,2,32,1024]{4,3,2,1,0:T(8,128)S(1)}, f32[1,2,2,32,1024]{4,3,2,1,0:T(8,128)S(1)}) fusion(bf16[4,2,2,32,1024]{4,3,2,1,0:T(8,128)(2,1)} %get-tuple-element.11), kind=kLoop, calls=%fused_computation.17 | loop fusion | bytes 4194304 | tf_op jit(solution)/shard_map/slice | solution.py:694
  117.8 0.9 bitcast_multiply_fusion.1
  118.6 0.1 bitcast_multiply_fusion
  118.7 1.0 copy.26
  119.7 0.0 copy-start.3
  119.7 1.0 copy.25
  120.7 0.0 copy-done.3
  120.7 0.0 copy-start.2
  120.7 0.8 copy.31
  121.5 0.4 copy-done.2
  121.9 0.8 copy.32
  (4 shorter events, 0.1 us)
Async XLA Ops:
  0.6 4.1 %copy-start = (bf16[128,1024]{1,0:T(8,128)(2,1)S(1)}, bf16[128,1024]{1,0:T(8,128)(2,1)}, u32[]{:S(2)}) copy-start(bf16[128,1024]{1,0:T(8,128)(2,1)} %param.24) | copy-start | bytes 786436
  0.6 4.1 %copy-start.4 = (bf16[1024,128]{1,0:T(8,128)(2,1)S(1)}, bf16[1024,128]{1,0:T(8,128)(2,1)}, u32[]{:S(2)}) copy-start(bf16[1024,128]{1,0:T(8,128)(2,1)} %param.23) | copy-start | bytes 786436
  4.9 1.0 copy-start.1
  5.9 1.0 copy-start.6
  5.9 1.0 copy-start.5
  119.7 1.0 copy-start.3
  120.7 1.2 %copy-start.2 = (bf16[256,1024]{1,0:T(8,128)(2,1)S(1)}, bf16[256,1024]{1,0:T(8,128)(2,1)}, u32[]{:S(2)}) copy-start(bf16[256,1024]{1,0:T(8,128)(2,1)} %get-tuple-element.10) | copy-start | bytes 1572868

commit v3 on v2

--- a/solution.py
+++ b/solution.py
@@ -121,15 +121,22 @@
 
 def kernel(
     nz,
-    q_ref,
-    k_ref,
-    v_ref,
-    tok_ref,
-    cot_ref,
     gain_ref,
-    io_ref,
-    w_hbm,
-    f_hbm,
+    fin_ref,
+    fout_ref,
+    fmid_ref,
+    fhid_ref,
+    *refs,
+):
+    args, refs = refs[:11], refs[11:]
+    run(nz, gain_ref, (fin_ref, fout_ref, fmid_ref, fhid_ref), args, *refs)
+
+
+def run(
+    nz,
+    gain_ref,
+    flips,
+    args,
     out_ref,
     grad_ref,
     sum_ref,
@@ -166,9 +173,14 @@
     core_s,
     core_r,
     local,
+    in_stage,
+    out_stage,
+    img_stage,
+    turned,
+    f_ref,
 ):
-    patches, width = tok_ref.shape
-    share = w_hbm.shape[1]
+    patches, width = out_ref.shape
+    share = w_all.shape[3]
     half = share // 2
     own_hidden = SIDE * SIDE * share
     band = min(256, own_hidden)
@@ -187,69 +199,41 @@
     greet = [
         partner,
         cross,
-        (z, c, lax.rem(x + 1, SIDE), y),
-        (z, c, lax.rem(x + 3, SIDE), y),
-        (z, c, x, lax.rem(y + 1, SIDE)),
-        (z, c, x, lax.rem(y + 3, SIDE)),
-    ] + [(lax.rem(z + d, nz), c, x, y) for d in range(1, nz)]
+        *[(lax.rem(z + d, nz), c, x, y) for d in range(1, nz)],
+    ]
+    plane = [
+        (lax.rem(x + d // SIDE, SIDE), lax.rem(y + d % SIDE, SIDE)) for d in range(1, SIDE * SIDE)
+    ]
+    greet += [(z, c, a, b) for a, b in plane]
     for device in greet:
         pl.semaphore_signal(barrier, inc=1, device_id=device, device_id_type=MESH_ID)
 
-    loads = [
-        pltpu.make_async_copy(w_hbm.at[m], w_all.at[m, x, y], local.at[m]) for m in range(4)
-    ] + [pltpu.make_async_copy(f_hbm, f_all.at[x, y], local.at[4])]
+    homes = [*(in_stage.at[i] for i in range(3)), *(out_stage.at[i] for i in range(3))]
+    homes += [*(img_stage.at[i] for i in range(4)), cot.at[pl.ds(0, patches)]]
+    loads = [pltpu.make_async_copy(arg, home, local.at[i]) for i, (arg, home) in enumerate(zip(args, homes))]
     for load in loads:
         load.start()
-    for load in loads:
+    q_ref, k_ref, v_ref, tok_ref = (img_stage.at[i] for i in range(4))
+    cot_ref = cot.at[pl.ds(0, patches)]
+    fin_ref, fout_ref, fmid_ref, fhid_ref = flips
+    images = fin_ref.shape[0]
+    for kind, ref in enumerate((fmid_ref, fhid_ref)):
+        table = ref[...].astype(F32)
+        for i in range(images):
+            f_ref[i, kind : kind + 1, :] = table[i : i + 1, :]
+    for load in loads[:6]:
         load.wait()
-    pl.semaphore_wait(barrier, len(greet))
-
-    def remote(slot, src, dst, device):
-        return pltpu.make_async_remote_copy(
-            src_ref=src,
-            dst_ref=dst,
-            send_sem=core_s.at[slot],
-            recv_sem=core_r.at[slot],
-            device_id=device,
-            device_id_type=MESH_ID,
-        )
-
-    def halves(n):
-        return lambda h: pl.ds(h * n, n)
-
-    rows_of = halves(half)
-    frows = halves(f_all.shape[2] // 2)
-
-    def gather_rings(m, base):
-        if m == 4:
-            first = Ring(at, "x", lambda j, h: f_all.at[j, y, frows(h)], ag_s, ag_r, base)
-            second = Ring(at, "y", lambda j, h: f_all.at[:, j, frows(h)], ag_s, ag_r, base + 6)
-        elif m % 2 == 0:
-            first = Ring(at, "x", lambda j, h: w_all.at[m, j, y, rows_of(h)], ag_s, ag_r, base)
-            second = Ring(at, "y", lambda j, h: w_all.at[m, :, j, rows_of(h)], ag_s, ag_r, base + 6)
-        else:
-            first = Ring(at, "y", lambda j, h: w_all.at[m, x, j, rows_of(h)], ag_s, ag_r, base)
-            second = Ring(at, "x", lambda j, h: w_all.at[m, j, :, rows_of(h)], ag_s, ag_r, base + 6)
-        return first, second
-
-    def slot_rows(i):
-        return pl.ds(i * patches, patches)
-
-    ag = [gather_rings(m, 12 * m) for m in range(5)]
-    sends = []
-
-    def send(slot, src, dst, device):
-        copy = remote(slot, src, dst, device)
-        copy.start()
-        sends.append(copy)
-        return copy
-
-    for m in (4, 0, 1):
-        ag[m][0].gather_start()
-    cot_1 = send(0, cot_ref, cot.at[slot_rows(1)], partner)
-    cot_2 = send(1, cot_ref, cot.at[slot_rows(2)], mate)
-    for m in (2, 3):
-        ag[m][0].gather_start()
+    mine_rows = pl.ds(pl.multiple_of((2 * c + zp) * share, share), share)
+    turned[0] = in_stage[0].T
+    turned[1] = (in_stage[1].astype(F32) * in_stage[2].astype(F32)).astype(BF).T
+    turned[2] = (out_stage[1].astype(F32) * out_stage[2].astype(F32)).astype(BF)
+    w_all[0, x, y] = turned[0, mine_rows, :]
+    w_all[1, x, y] = turned[1, mine_rows, :]
+    w_all[2, x, y] = out_stage[0, mine_rows, :]
+    w_all[3, x, y] = turned[2, mine_rows, :]
+    f_all[x, y] = f_ref[s]
+    for load in loads[6:]:
+        load.wait()
 
     def attend(p):
         lanes = pl.ds(pl.multiple_of(p * 128, 128), 128)
@@ -266,23 +250,104 @@
 
     pairs = width // 128
 
-    @pl.loop(0, pairs // 2)
-    def _(p):
-        attend(p)
-
-    for m in (4, 0, 1, 2, 3):
+    def attend_span(k):
+        @pl.loop(k * pairs // 4, (k + 1) * pairs // 4)
+        def _(p):
+            attend(p)
+
+    attend_span(0)
+    pl.semaphore_wait(barrier, len(greet))
+
+    def remote(slot, src, dst, device):
+        return pltpu.make_async_remote_copy(
+            src_ref=src,
+            dst_ref=dst,
+            send_sem=core_s.at[slot],
+            recv_sem=core_r.at[slot],
+            device_id=device,
+            device_id_type=MESH_ID,
+        )
+
+    def halves(n):
+        return lambda h: pl.ds(h * n, n)
+
+    rows_of = halves(half)
+
+    def gather_rings(m, base):
+        if m % 2 == 0:
+            first = Ring(at, "x", lambda j, h: w_all.at[m, j, y, rows_of(h)], ag_s, ag_r, base)
+            second = Ring(at, "y", lambda j, h: w_all.at[m, :, j, rows_of(h)], ag_s, ag_r, base + 6)
+        else:
+            first = Ring(at, "y", lambda j, h: w_all.at[m, x, j, rows_of(h)], ag_s, ag_r, base)
+            second = Ring(at, "x", lambda j, h: w_all.at[m, j, :, rows_of(h)], ag_s, ag_r, base + 6)
+        return first, second
+
+    def slot_rows(i):
+        return pl.ds(i * patches, patches)
+
+    ag = [gather_rings(m, 12 * m) for m in range(4)]
+    sends = []
+
+    def send(src, dst, device):
+        copy = remote(len(sends), src, dst, device)
+        copy.start()
+        sends.append(copy)
+        return copy
+
+    for m in (0, 1):
+        ag[m][0].gather_start()
+    half_rows = [pl.ds(h * (patches // 2), patches // 2) for h in range(2)]
+
+    def half_slot(i, h):
+        return cot.at[pl.ds(i * patches + h * (patches // 2), patches // 2)]
+
+    cot_2 = [send(cot_ref.at[half_rows[0]], half_slot(2, 0), mate)]
+    tables = [
+        send(f_ref.at[a * SIDE + b], f_all.at[x, y], (z, c, a, b)) for a, b in plane
+    ]
+    for m in (2, 3):
+        ag[m][0].gather_start()
+    cot_1 = send(cot_ref, cot.at[slot_rows(1)], partner)
+
+    attend_span(1)
+    for m in (0, 1):
         ag[m][0].gather_forward()
-
-    @pl.loop(pairs // 2, pairs)
-    def _(p):
-        attend(p)
-
-    for m in (4, 0, 1):
+    attend_span(2)
+    for m in (2, 3):
+        ag[m][0].gather_forward()
+    for m in (0, 1):
         ag[m][0].gather_finish()
         ag[m][1].gather_start()
 
+    for copy in tables:
+        copy.wait_recv()
+    def own_row(t):
+        keep = lax.broadcasted_iota(jnp.int32, t.shape, 0) == s
+        return jnp.sum(jnp.where(keep, t.astype(F32), 0.0), axis=0, keepdims=True)
+
+    for row, ref in enumerate((fin_ref, fout_ref)):
+        own = own_row(ref[...])
+        for t in range(4):
+            msg[t, row : row + 1, 0:width] = own
+    for a in range(SIDE):
+        picked = [f_all[a, b] for b in range(SIDE)]
+        for t in range(4):
+            for kind in range(2):
+                lo = t * share
+                first = kind * own_hidden + a * SIDE * share
+                msg[t, 2:3, first : first + SIDE * share] = jnp.concatenate(
+                    [row[kind : kind + 1, lo : lo + share] for row in picked], axis=1
+                )
+    quarter = lambda core, parity: msg.at[2 * core + parity]
+    sign_1 = send(quarter(1 - c, zp), signs.at[1], partner)
+    sign_2 = send(quarter(c, 1 - zp), signs.at[2], mate)
+    sign_3 = send(quarter(1 - c, 1 - zp), signs.at[3], cross)
+    signs[0] = msg[2 * c + zp]
+
+    attend_span(3)
+
     chunk = min(64, patches)
-    gain = gain_ref[...].astype(F32)
+    gain = gain_ref[...].astype(F32).reshape(1, width)
 
     def stats(r):
         xf = resid[r, :].astype(F32)
@@ -295,36 +360,12 @@
         r = pl.ds(pl.multiple_of(i * chunk, chunk), chunk)
         _, ahat, _ = stats(r)
         norm[r, :] = (ahat * gain).astype(BF)
-        cot[r, :] = cot_ref[r, :]
-
+
+    norm_1 = send(norm.at[slot_rows(0)], norm.at[slot_rows(1)], partner)
+    norm_2 = send(norm.at[slot_rows(0)], norm.at[slot_rows(2)], mate)
+    cot_2.append(send(cot_ref.at[half_rows[1]], half_slot(2, 1), mate))
     for m in (2, 3):
         ag[m][0].gather_finish()
-        ag[m][1].gather_start()
-    norm_1 = send(3, norm.at[slot_rows(0)], norm.at[slot_rows(1)], partner)
-    norm_2 = send(4, norm.at[slot_rows(0)], norm.at[slot_rows(2)], mate)
-    ag[4][1].gather_forward()
-    ag[4][1].gather_finish()
-
-    def own_row(t):
-        keep = lax.broadcasted_iota(jnp.int32, t.shape, 0) == s
-        return jnp.sum(jnp.where(keep, t, 0.0), axis=0, keepdims=True)
-
-    for t in range(4):
-        msg[t, 0:2, 0:width] = io_ref[0:2, :]
-    for a in range(SIDE):
-        picked = [own_row(f_all[a, b]) for b in range(SIDE)]
-        for t in range(4):
-            for kind in range(2):
-                lo = (kind * 4 + t) * share
-                first = kind * own_hidden + a * SIDE * share
-                msg[t, 2:3, first : first + SIDE * share] = jnp.concatenate(
-                    [row[:, lo : lo + share] for row in picked], axis=1
-                )
-    quarter = lambda core, parity: msg.at[2 * core + parity]
-    sign_1 = send(6, quarter(1 - c, zp), signs.at[1], partner)
-    sign_2 = send(7, quarter(c, 1 - zp), signs.at[2], mate)
-    sign_3 = send(8, quarter(1 - c, 1 - zp), signs.at[3], cross)
-    signs[0] = msg[2 * c + zp]
 
     def flip(dst, src, slot, row):
         @pl.loop(0, patches // chunk)
@@ -332,18 +373,18 @@
             r = pl.ds(pl.multiple_of(slot * patches + i * chunk, chunk), chunk)
             dst[r, :] = src[r, :] * signs[slot, row : row + 1, 0:width].astype(BF)
 
+    flip(norm_f, norm, 0, 0)
+    flip(cot_f, cot, 0, 1)
     for m in (0, 1):
         ag[m][1].gather_forward()
-    flip(norm_f, norm, 0, 0)
-    flip(cot_f, cot, 0, 1)
+    for m in (2, 3):
+        ag[m][1].gather_start()
     for copy in (cot_1, norm_1, sign_1):
         copy.wait_recv()
     flip(norm_f, norm, 1, 0)
     flip(cot_f, cot, 1, 1)
-    for m in (2, 3):
-        ag[m][1].gather_forward()
-    cot_2.wait_recv()
-    cot_3 = send(2, cot.at[slot_rows(2)], cot.at[slot_rows(3)], partner)
+    cot_2[0].wait_recv()
+    cot_3 = [send(half_slot(2, 0), half_slot(3, 0), partner)]
     for m in (0, 1):
         ag[m][1].gather_finish()
 
@@ -448,18 +489,26 @@
             z_live[m, 0, d].wait_recv()
             acc = acc + zbuf[m, d - 1].astype(F32)
         total[m, c, zp, r, l] = acc.astype(BF)
-        for d in range(1, nz):
+        for d in range(1, nk):
             place = total.at[m, c, zp, r, l]
-            z_copy(m, 1, d, 1, place, place)
-
-    z_last = {}
+            z_copy(m, 1, d, 2, place, place)
+
+    beside = (lax.rem(z + nz - 1 + 2 * zp, nz), c, x, y)
+    last = {}
+
+    def z_hand(m):
+        for d in range(1, nk):
+            z_live[m, 1, d].wait_recv()
+        own = total.at[m, c, zp]
+        last[m, 0] = send(own, own, beside)
+        last[m, 1] = send(own, own, partner)
 
     def z_finish(m):
-        for d in range(1, nz):
-            z_live[m, 1, d].wait_recv()
-        z_last[m] = send(15 + m, total.at[m, c], total.at[m, c], partner)
-
-    def project(left, left_f, t, sign):
+        last[m, 0].wait_recv()
+        far = total.at[m, c, 1 - zp]
+        last[m, 2] = send(far, far, partner)
+
+    def project(left, left_f, t, sign, slots):
         m = 2 * t
 
         @pl.loop(0, width // nblk)
@@ -467,7 +516,7 @@
             lanes = pl.ds(pl.multiple_of(n * nblk, nblk), nblk)
             plain = w_all[m, :, :, :, lanes].reshape(own_hidden, nblk)
             noisy = w_all[m + 1, :, :, :, lanes].reshape(own_hidden, nblk)
-            for i in range(4):
+            for i in slots:
                 r = slice(i * patches, (i + 1) * patches)
                 out = dot_n(left[r, :], plain)
                 out = out + dot_n(left_f[r, :], noisy) * signs[i, sign : sign + 1, lanes]
@@ -476,11 +525,6 @@
                 else:
                     mine[t, :, lanes] = out
 
-        base = 12 - 3 * t
-        to_pair = send(base, theirs.at[t, 0], arrived.at[t, 0], partner)
-        to_far = send(base + 1, theirs.at[t, 2], arrived.at[t, 1], partner)
-        return to_pair, to_far
-
     def relay(t, to_far):
         to_far.wait_recv()
 
@@ -490,73 +534,93 @@
             both = theirs[t, 1, r, :].astype(F32) + arrived[t, 1, r, :].astype(F32)
             theirs[t, 1, r, :] = both.astype(BF)
 
-        return send(14 - 3 * t, theirs.at[t, 1], arrived.at[t, 2], mate)
+        return send(theirs.at[t, 1], arrived.at[t, 2], mate)
 
     forward(0, 2)
+    for m in (2, 3):
+        ag[m][1].gather_forward()
     sign_2.wait_recv()
-    flip(cot_f, cot, 2, 1)
     norm_2.wait_recv()
-    norm_3 = send(5, norm.at[slot_rows(2)], norm.at[slot_rows(3)], partner)
+    norm_3 = send(norm.at[slot_rows(2)], norm.at[slot_rows(3)], partner)
     flip(norm_f, norm, 2, 0)
     forward(2, 3)
     sign_3.wait_recv()
-    cot_3.wait_recv()
-    flip(cot_f, cot, 3, 1)
     norm_3.wait_recv()
     flip(norm_f, norm, 3, 0)
     forward(3, 4)
+    for m in (2, 3):
+        ag[m][1].gather_finish()
+    project(hid, hid_f, 1, 1, (2, 3))
+    mixed_far = send(theirs.at[1, 2], arrived.at[1, 1], partner)
+    cot_2[1].wait_recv()
+    cot_3.append(send(half_slot(2, 1), half_slot(3, 1), partner))
+    flip(cot_f, cot, 2, 1)
+    mixed_2 = relay(1, mixed_far)
+    for copy in cot_3:
+        copy.wait_recv()
+    flip(cot_f, cot, 3, 1)
     weight_grad(2, hid, cot)
     start1(2)
     weight_grad(3, hid_f, cot_f)
     start1(3)
-    for m in (2, 3):
-        ag[m][1].gather_finish()
-    mixed_1, mixed_far = project(hid, hid_f, 1, 1)
     backward(0, 4)
-    mixed_2 = relay(1, mixed_far)
-    for m in (2, 3):
-        rs[m][0].scatter_forward(add_into)
+    rs[2][0].scatter_forward(add_into)
     weight_grad(0, dpre, norm)
     start1(0)
+    rs[3][0].scatter_forward(add_into)
     weight_grad(1, dpre_f, norm_f)
     start1(1)
-    for m in (2, 3):
+    project(dpre, dpre_f, 0, 0, (2, 3))
+    back_far = send(theirs.at[0, 2], arrived.at[0, 1], partner)
+
+    def finish1(m):
         rs[m][0].scatter_finish(add_into)
         start2(m)
-    back_1, back_far = project(dpre, dpre_f, 0, 0)
-    for m in (0, 1):
+
+    def forward1(m):
         rs[m][0].scatter_forward(add_into)
-    back_2 = relay(0, back_far)
-    for m in (2, 3):
+
+    def forward2(m):
         rs[m][1].scatter_forward(add_into)
-    for m in (0, 1):
-        rs[m][0].scatter_finish(add_into)
-        start2(m)
-    for m in (2, 3):
+
+    def finish2(m):
         rs[m][1].scatter_finish(add_into)
         z_start(m)
-    for m in (0, 1):
-        rs[m][1].scatter_forward(add_into)
-    for m in (2, 3):
-        z_spread(m)
+
+    def gathered(t, r):
+        return mine[t, r, :] + arrived[t, 0, r, :].astype(F32) + arrived[t, 2, r, :].astype(F32)
+
+    finish1(2)
+    back_2 = relay(0, back_far)
+    finish1(3)
+    project(hid, hid_f, 1, 1, (0, 1))
+    mixed_1 = send(theirs.at[1, 0], arrived.at[1, 0], partner)
+    forward1(0)
+    forward2(2)
+    project(dpre, dpre_f, 0, 0, (0, 1))
+    back_1 = send(theirs.at[0, 0], arrived.at[0, 0], partner)
+    forward2(3)
+    forward1(1)
+    finish2(2)
+    finish2(3)
+    finish1(0)
     mixed_1.wait_recv()
     mixed_2.wait_recv()
-
-    def gathered(t, r):
-        return mine[t, r, :] + arrived[t, 0, r, :].astype(F32) + arrived[t, 2, r, :].astype(F32)
 
     @pl.loop(0, patches // chunk)
     def _(i):
         r = pl.ds(pl.multiple_of(i * chunk, chunk), chunk)
         out_ref[r, :] = (resid[r, :].astype(F32) + gathered(1, r)).astype(BF)
 
-    for m in (0, 1):
-        rs[m][1].scatter_finish(add_into)
-        z_start(m)
-    for m in (2, 3):
-        z_finish(m)
-    for m in (0, 1):
-        z_spread(m)
+    finish1(1)
+    forward2(0)
+    forward2(1)
+    finish2(0)
+    finish2(1)
+    z_spread(2)
+    z_spread(3)
+    z_spread(0)
+    z_spread(1)
     back_1.wait_recv()
     back_2.wait_recv()
 
@@ -572,11 +636,20 @@
         )
         grad_ref[r, :] = (cot_ref[r, :].astype(F32) + back).astype(BF)
 
+    for m in (2, 3, 0, 1):
+        z_hand(m)
+    z_finish(2)
+    z_finish(3)
+    for m in (2, 3):
+        last[m, 1].wait_recv()
+        last[m, 2].wait_recv()
+        sum_ref[m] = total[m]
+    z_finish(0)
+    z_finish(1)
     for m in (0, 1):
-        z_finish(m)
-    for m in (2, 3, 0, 1):
-        z_last[m].wait_recv()
-    sum_ref[...] = total[...]
+        last[m, 1].wait_recv()
+        last[m, 2].wait_recv()
+        sum_ref[m] = total[m]
 
     for first, second in ag + rs:
         first.drain()
@@ -585,9 +658,11 @@
         copy.wait_send()
 
 
-def layer(q, k, v, tok, cot, gain, io, w, f, nz):
-    patches, width = tok.shape
-    share = w.shape[1]
+def layer(gain, flips, mats, images, nz):
+    patches, width = images[0].shape
+    cols = mats[0].shape[1]
+    share = cols // 4
+    count = flips[0].shape[0]
     half = share // 2
     hidden = SIDE * SIDE * share
     four = 4 * patches
@@ -599,7 +674,7 @@
     dma = pltpu.SemaphoreType.DMA
     scratch = [
         pltpu.VMEM((4, SIDE, SIDE, share, width), BF),
-        pltpu.VMEM((SIDE, SIDE, *f.shape), F32),
+        pltpu.VMEM((SIDE, SIDE, 8, cols), F32),
         pltpu.VMEM((4, 8, max(width, 2 * hidden)), F32),
         pltpu.VMEM((4, 8, max(width, 2 * hidden)), F32),
         pltpu.VMEM((four, width), BF),
@@ -622,15 +697,20 @@
         pltpu.VMEM((4, 4, half, width), BF),
         pltpu.VMEM((4, nk - 1, zr, zl), BF),
         pltpu.VMEM((4, 2, 2, share, width), BF),
-        dma((60,)),
-        dma((60,)),
         dma((48,)),
         dma((48,)),
-        dma((4, 2, nz - 1)),
-        dma((4, 2, nz - 1)),
-        dma((19,)),
-        dma((19,)),
-        dma((5,)),
+        dma((48,)),
+        dma((48,)),
+        dma((4, 2, nk - 1)),
+        dma((4, 2, nk - 1)),
+        dma((44,)),
+        dma((44,)),
+        dma((11,)),
+        pltpu.VMEM((3, width, cols), BF),
+        pltpu.VMEM((3, cols, width), BF),
+        pltpu.VMEM((4, patches, width), BF),
+        pltpu.VMEM((3, cols, width), BF),
+        pltpu.VMEM((count, 8, cols), F32),
     ]
     return pl.pallas_call(
         functools.partial(kernel, nz),
@@ -639,14 +719,14 @@
             jax.ShapeDtypeStruct((patches, width), BF),
             jax.ShapeDtypeStruct((4, 2, 2, share, width), BF),
         ),
-        in_specs=[vmem] * 7 + [any_space] * 2,
+        in_specs=[vmem] * 5 + [any_space] * 11,
         out_specs=(vmem, vmem, vmem),
         scratch_shapes=scratch,
         compiler_params=pltpu.CompilerParams(
             collective_id=0, has_side_effects=True, vmem_limit_bytes=62 * 1024 * 1024
         ),
         name="layer",
-    )(q, k, v, tok, cot, gain, io, w, f)
+    )(gain, *flips, *mats, *images)
 
 
 def body(
@@ -669,25 +749,15 @@
 ):
     nz = lax.axis_size("z")
     width = tokens.shape[-1]
-    share = mean_in.shape[1] // 4
-    quarter = lax.axis_index("c") * 2 + lax.rem(lax.axis_index("z"), 2)
-    s = lax.axis_index("x") * SIDE + lax.axis_index("y")
-    pert_in = (sigma_in.astype(F32) * noise_in.astype(F32)).astype(BF)
-    pert_out = (sigma_out.astype(F32) * noise_out.astype(F32)).astype(BF)
-
-    def own(t, axis):
-        return lax.dynamic_slice_in_dim(t, quarter * share, share, axis)
-
-    w = jnp.stack([own(mean_in, 1).T, own(pert_in, 1).T, own(mean_out, 0), own(pert_out, 0)])
-    f = jnp.concatenate([flip_mid, flip_hidden], axis=1).astype(F32)
-    io = jnp.stack(
-        [lax.dynamic_index_in_dim(t, s, 0, False).astype(F32) for t in (flip_in, flip_out)]
+    cols = mean_in.shape[1]
+    out, grad, sums = layer(
+        ln_gain,
+        (flip_in, flip_out, flip_mid, flip_hidden),
+        (mean_in, sigma_in, noise_in, mean_out, sigma_out, noise_out),
+        (queries[0], keys[0], values[0], tokens[0], cotangent[0]),
+        nz,
     )
-    io = jnp.pad(io, ((0, 6), (0, 0)))
-    out, grad, sums = layer(
-        queries[0], keys[0], values[0], tokens[0], cotangent[0], ln_gain.reshape(1, width), io, w, f, nz
-    )
-    sums = sums.astype(F32).reshape(4, 4 * share, width)
+    sums = sums.astype(F32).reshape(4, cols, width)
     grad_mean_in = sums[0].T
     grad_sigma_in = sums[1].T * noise_in.astype(F32)
     grad_mean_out = sums[2]

time: 123 us -> 106 us (0.86)
  Pallas kernels: 107 us -> 96.9 us
  other arithmetic: 5.4 us -> 1.69 us
  local copies, waits for them, and re-layouts: 9.22 us -> 6.28 us
    pallas_call x1, Pallas kernels: 107 us -> 96.9 us  [layer(): pl.pallas_call(functools.partial(kernel, nz), out_shape=(jax.ShapeDtypeSt...]
    another operation x4 -> x0, other arithmetic: 2.3 us -> none  [the longest x3 1.67 us: body(): jnp.stack([own(mean_in, 1).T, own(pert_in, 1).T, own(mean_out, 0), own(pe...]
    convert_element_type x4 -> x0, other arithmetic: 2.19 us -> none  [the longest x1 1.32 us: body(): f = jnp.concatenate([flip_mid, flip_hidden], axis=1).astype(F32)]
    unnamed x20 -> x10, local copies, waits for them, and re-layouts: 4.45 us -> 2.83 us
    reshape x1 -> x0, local copies, waits for them, and re-layouts: 1.33 us -> none  [body(): ln_gain.reshape(1, width)]
where the time goes in v3:
time: 106 us; the launch traced here: 105 us
  Pallas kernels  96.9 us (91%)
  local copies, waits for them, and re-layouts  6.28 us (6%)
  other arithmetic  1.69 us (2%)
    pallas_call x1, Pallas kernels, layer(): pl.pallas_call(functools.partial(kernel, nz), out_shape=(jax.ShapeDtypeSt...  96.9 us
    unnamed x10, local copies, waits for them, and re-layouts  2.83 us
    slice x1, local copies, waits for them, and re-layouts, body(): grad_sigma_out = sums[3] * noise_out.astype(F32)  2.27 us

profile of v3, /device:TPU:1, one launch (start us, length us, event | category | flops | bytes accessed | tf_op | source)
XLA Modules:
  0.0 105.5 jit_solution(1146999369140619967)
XLA Ops:
  0.6 96.9 %layer.1 = (bf16[256,1024]{1,0:T(8,128)(2,1)}, bf16[256,1024]{1,0:T(8,128)(2,1)}, bf16[4,2,2,32,1024]{4,3,2,1,0:T(8,128)(2,1)}) custom-call(bf16[1024]{0:T(1024)(128)(2,1)} %gain_ref.1, s32[16,1024]{1,0:T(8,128)} %fin_ref.1, s32[16,1024]{1,0:T(8,128)} %fout_ref.1, s32[16,128]{1,0:T(8,128)} %fmid_ref.1, s32[16,128]{1,0:T(8,128)} %fhid_ref.1, ...), custom_call_target="tpu_custom_call" | custom-call | tf_op jit(solution)/shard_map/layer/pallas_call | solution.py:715
  97.5 0.0 copy-start
  97.5 2.3 %fusion = (f32[1,2,2,32,1024]{4,3,2,1,0:T(8,128)S(1)}, f32[1,2,2,32,1024]{4,3,2,1,0:T(8,128)}, f32[1,2,2,32,1024]{4,3,2,1,0:T(8,128)S(1)}, f32[1,2,2,32,1024]{4,3,2,1,0:T(8,128)S(1)}) fusion(bf16[4,2,2,32,1024]{4,3,2,1,0:T(8,128)(2,1)} %get-tuple-element.11), kind=kLoop, calls=%fused_computation.2 | loop fusion | bytes 4194304 | tf_op jit(solution)/shard_map/slice | solution.py:764
  99.8 0.0 copy-done
  99.8 0.9 bitcast_multiply_fusion
  100.6 0.0 copy-start.1
  100.6 0.2 copy.23
  100.8 0.8 copy-done.1
  101.6 0.8 bitcast_multiply_fusion.1
  102.4 0.0 copy-start.3
  102.4 1.0 copy.22
  103.4 0.0 copy-done.3
  103.5 0.0 copy-start.2
  103.5 0.8 copy.26
  104.3 0.4 copy-done.2
  104.7 0.8 copy.27
Async XLA Ops:
  97.5 2.3 %copy-start = (bf16[128,1024]{1,0:T(8,128)(2,1)S(1)}, bf16[128,1024]{1,0:T(8,128)(2,1)}, u32[]{:S(2)}) copy-start(bf16[128,1024]{1,0:T(8,128)(2,1)} %refs_5_.1) | copy-start | bytes 786436
  100.6 0.9 copy-start.1
  102.4 1.0 copy-start.3
  103.5 1.2 %copy-start.2 = (bf16[256,1024]{1,0:T(8,128)(2,1)S(1)}, bf16[256,1024]{1,0:T(8,128)(2,1)}, u32[]{:S(2)}) copy-start(bf16[256,1024]{1,0:T(8,128)(2,1)} %get-tuple-element.10) | copy-start | bytes 1572868

commit v4 on v3

--- a/solution.py
+++ b/solution.py
@@ -139,7 +139,10 @@
     args,
     out_ref,
     grad_ref,
-    sum_ref,
+    mean_in_ref,
+    sigma_in_ref,
+    mean_out_ref,
+    sigma_out_ref,
     w_all,
     f_all,
     msg,
@@ -294,27 +297,44 @@
         sends.append(copy)
         return copy
 
-    for m in (0, 1):
-        ag[m][0].gather_start()
-    half_rows = [pl.ds(h * (patches // 2), patches // 2) for h in range(2)]
-
-    def half_slot(i, h):
-        return cot.at[pl.ds(i * patches + h * (patches // 2), patches // 2)]
-
-    cot_2 = [send(cot_ref.at[half_rows[0]], half_slot(2, 0), mate)]
     tables = [
         send(f_ref.at[a * SIDE + b], f_all.at[x, y], (z, c, a, b)) for a, b in plane
     ]
-    for m in (2, 3):
+    for m in range(4):
         ag[m][0].gather_start()
+    half_rows = [pl.ds(h * (patches // 2), patches // 2) for h in range(2)]
+
+    def half_slot(i, h):
+        return cot.at[pl.ds(i * patches + h * (patches // 2), patches // 2)]
+
+    cot_2 = [send(cot_ref.at[half_rows[0]], half_slot(2, 0), mate)]
     cot_1 = send(cot_ref, cot.at[slot_rows(1)], partner)
 
     attend_span(1)
+    attend_span(2)
     for m in (0, 1):
         ag[m][0].gather_forward()
-    attend_span(2)
+    attend_span(3)
     for m in (2, 3):
         ag[m][0].gather_forward()
+
+    chunk = min(64, patches)
+    gain = gain_ref[...].astype(F32).reshape(1, width)
+
+    def stats(r):
+        xf = resid[r, :].astype(F32)
+        centered = xf - jnp.mean(xf, axis=-1, keepdims=True)
+        rstd = lax.rsqrt(jnp.mean(centered * centered, axis=-1, keepdims=True) + 1e-06)
+        return xf, centered * rstd, rstd
+
+    @pl.loop(0, patches // chunk)
+    def _(i):
+        r = pl.ds(pl.multiple_of(i * chunk, chunk), chunk)
+        _, ahat, _ = stats(r)
+        norm[r, :] = (ahat * gain).astype(BF)
+
+    norm_1 = send(norm.at[slot_rows(0)], norm.at[slot_rows(1)], partner)
+    norm_2 = send(norm.at[slot_rows(0)], norm.at[slot_rows(2)], mate)
     for m in (0, 1):
         ag[m][0].gather_finish()
         ag[m][1].gather_start()
@@ -343,29 +363,7 @@
     sign_2 = send(quarter(c, 1 - zp), signs.at[2], mate)
     sign_3 = send(quarter(1 - c, 1 - zp), signs.at[3], cross)
     signs[0] = msg[2 * c + zp]
-
-    attend_span(3)
-
-    chunk = min(64, patches)
-    gain = gain_ref[...].astype(F32).reshape(1, width)
-
-    def stats(r):
-        xf = resid[r, :].astype(F32)
-        centered = xf - jnp.mean(xf, axis=-1, keepdims=True)
-        rstd = lax.rsqrt(jnp.mean(centered * centered, axis=-1, keepdims=True) + 1e-06)
-        return xf, centered * rstd, rstd
-
-    @pl.loop(0, patches // chunk)
-    def _(i):
-        r = pl.ds(pl.multiple_of(i * chunk, chunk), chunk)
-        _, ahat, _ = stats(r)
-        norm[r, :] = (ahat * gain).astype(BF)
-
-    norm_1 = send(norm.at[slot_rows(0)], norm.at[slot_rows(1)], partner)
-    norm_2 = send(norm.at[slot_rows(0)], norm.at[slot_rows(2)], mate)
     cot_2.append(send(cot_ref.at[half_rows[1]], half_slot(2, 1), mate))
-    for m in (2, 3):
-        ag[m][0].gather_finish()
 
     def flip(dst, src, slot, row):
         @pl.loop(0, patches // chunk)
@@ -375,6 +373,8 @@
 
     flip(norm_f, norm, 0, 0)
     flip(cot_f, cot, 0, 1)
+    for m in (2, 3):
+        ag[m][0].gather_finish()
     for m in (0, 1):
         ag[m][1].gather_forward()
     for m in (2, 3):
@@ -502,6 +502,12 @@
         own = total.at[m, c, zp]
         last[m, 0] = send(own, own, beside)
         last[m, 1] = send(own, own, partner)
+
+    sum_refs = (mean_in_ref, sigma_in_ref, mean_out_ref, sigma_out_ref)
+
+    def flat_sum(m):
+        flat = total[m].reshape(4 * share, width)
+        return flat.T if m < 2 else flat
 
     def z_finish(m):
         last[m, 0].wait_recv()
@@ -537,32 +543,32 @@
         return send(theirs.at[t, 1], arrived.at[t, 2], mate)
 
     forward(0, 2)
-    for m in (2, 3):
-        ag[m][1].gather_forward()
     sign_2.wait_recv()
     norm_2.wait_recv()
     norm_3 = send(norm.at[slot_rows(2)], norm.at[slot_rows(3)], partner)
     flip(norm_f, norm, 2, 0)
     forward(2, 3)
+    for m in (2, 3):
+        ag[m][1].gather_forward()
     sign_3.wait_recv()
     norm_3.wait_recv()
     flip(norm_f, norm, 3, 0)
     forward(3, 4)
+    cot_2[1].wait_recv()
+    cot_3.append(send(half_slot(2, 1), half_slot(3, 1), partner))
+    flip(cot_f, cot, 2, 1)
+    for copy in cot_3:
+        copy.wait_recv()
+    weight_grad(2, hid, cot)
+    start1(2)
     for m in (2, 3):
         ag[m][1].gather_finish()
     project(hid, hid_f, 1, 1, (2, 3))
     mixed_far = send(theirs.at[1, 2], arrived.at[1, 1], partner)
-    cot_2[1].wait_recv()
-    cot_3.append(send(half_slot(2, 1), half_slot(3, 1), partner))
-    flip(cot_f, cot, 2, 1)
-    mixed_2 = relay(1, mixed_far)
-    for copy in cot_3:
-        copy.wait_recv()
     flip(cot_f, cot, 3, 1)
-    weight_grad(2, hid, cot)
-    start1(2)
     weight_grad(3, hid_f, cot_f)
     start1(3)
+    mixed_2 = relay(1, mixed_far)
     backward(0, 4)
     rs[2][0].scatter_forward(add_into)
     weight_grad(0, dpre, norm)
@@ -590,20 +596,27 @@
     def gathered(t, r):
         return mine[t, r, :] + arrived[t, 0, r, :].astype(F32) + arrived[t, 2, r, :].astype(F32)
 
+    forward1(0)
     finish1(2)
     back_2 = relay(0, back_far)
+    forward1(1)
     finish1(3)
     project(hid, hid_f, 1, 1, (0, 1))
     mixed_1 = send(theirs.at[1, 0], arrived.at[1, 0], partner)
-    forward1(0)
+    finish1(0)
+    finish1(1)
     forward2(2)
+    forward2(3)
+    forward2(0)
+    forward2(1)
+    finish2(2)
+    finish2(3)
+    finish2(0)
+    finish2(1)
     project(dpre, dpre_f, 0, 0, (0, 1))
     back_1 = send(theirs.at[0, 0], arrived.at[0, 0], partner)
-    forward2(3)
-    forward1(1)
-    finish2(2)
-    finish2(3)
-    finish1(0)
+    z_spread(2)
+    z_spread(3)
     mixed_1.wait_recv()
     mixed_2.wait_recv()
 
@@ -612,15 +625,10 @@
         r = pl.ds(pl.multiple_of(i * chunk, chunk), chunk)
         out_ref[r, :] = (resid[r, :].astype(F32) + gathered(1, r)).astype(BF)
 
-    finish1(1)
-    forward2(0)
-    forward2(1)
-    finish2(0)
-    finish2(1)
-    z_spread(2)
-    z_spread(3)
     z_spread(0)
     z_spread(1)
+    z_hand(2)
+    z_hand(3)
     back_1.wait_recv()
     back_2.wait_recv()
 
@@ -636,20 +644,20 @@
         )
         grad_ref[r, :] = (cot_ref[r, :].astype(F32) + back).astype(BF)
 
-    for m in (2, 3, 0, 1):
-        z_hand(m)
+    z_hand(0)
+    z_hand(1)
     z_finish(2)
     z_finish(3)
     for m in (2, 3):
         last[m, 1].wait_recv()
         last[m, 2].wait_recv()
-        sum_ref[m] = total[m]
+        sum_refs[m][...] = flat_sum(m)
     z_finish(0)
     z_finish(1)
     for m in (0, 1):
         last[m, 1].wait_recv()
         last[m, 2].wait_recv()
-        sum_ref[m] = total[m]
+        sum_refs[m][...] = flat_sum(m)
 
     for first, second in ag + rs:
         first.drain()
@@ -717,10 +725,13 @@
         out_shape=(
             jax.ShapeDtypeStruct((patches, width), BF),
             jax.ShapeDtypeStruct((patches, width), BF),
-            jax.ShapeDtypeStruct((4, 2, 2, share, width), BF),
+            jax.ShapeDtypeStruct((width, cols), BF),
+            jax.ShapeDtypeStruct((width, cols), BF),
+            jax.ShapeDtypeStruct((cols, width), BF),
+            jax.ShapeDtypeStruct((cols, width), BF),
         ),
         in_specs=[vmem] * 5 + [any_space] * 11,
-        out_specs=(vmem, vmem, vmem),
+        out_specs=(vmem,) * 6,
         scratch_shapes=scratch,
         compiler_params=pltpu.CompilerParams(
             collective_id=0, has_side_effects=True, vmem_limit_bytes=62 * 1024 * 1024
@@ -748,20 +759,16 @@
     cotangent,
 ):
     nz = lax.axis_size("z")
-    width = tokens.shape[-1]
-    cols = mean_in.shape[1]
-    out, grad, sums = layer(
+    out, grad, *sums = layer(
         ln_gain,
         (flip_in, flip_out, flip_mid, flip_hidden),
         (mean_in, sigma_in, noise_in, mean_out, sigma_out, noise_out),
         (queries[0], keys[0], values[0], tokens[0], cotangent[0]),
         nz,
     )
-    sums = sums.astype(F32).reshape(4, cols, width)
-    grad_mean_in = sums[0].T
-    grad_sigma_in = sums[1].T * noise_in.astype(F32)
-    grad_mean_out = sums[2]
-    grad_sigma_out = sums[3] * noise_out.astype(F32)
+    grad_mean_in, grad_sigma_in, grad_mean_out, grad_sigma_out = (t.astype(F32) for t in sums)
+    grad_sigma_in = grad_sigma_in * noise_in.astype(F32)
+    grad_sigma_out = grad_sigma_out * noise_out.astype(F32)
     return out[None], grad[None], grad_mean_in, grad_sigma_in, grad_mean_out, grad_sigma_out
 
 

time: 106 us -> 103 us (0.972)
  local copies, waits for them, and re-layouts: 6.28 us -> 2.91 us
  other arithmetic: 1.69 us -> 4.38 us
  Pallas kernels: 96.9 us -> 94.4 us
    convert_element_type x0 -> x2, other arithmetic: none -> 2.67 us  [body(): t.astype(F32)]
    pallas_call x1, Pallas kernels: 96.9 us -> 94.4 us  [layer(): pl.pallas_call(functools.partial(kernel, nz), out_shape=(jax.ShapeDtypeSt...]
    slice x1 -> x0, local copies, waits for them, and re-layouts: 2.27 us -> none  [body(): grad_sigma_out = sums[3] * noise_out.astype(F32)]
    squeeze x2 -> x0, local copies, waits for them, and re-layouts: 1.18 us -> none  [the longest x1 0.99 us: body(): grad_mean_in = sums[0].T]
    unnamed x10 -> x16, local copies, waits for them, and re-layouts: 2.83 us -> 2.91 us
where the time goes in v4:
time: 103 us; the launch traced here: 102 us
  Pallas kernels  94.4 us (92%)
  other arithmetic  4.38 us (4%)
  local copies, waits for them, and re-layouts  2.91 us (3%)
    pallas_call x1, Pallas kernels, layer(): pl.pallas_call(functools.partial(kernel, nz), out_shape=(jax.ShapeDtypeSt...  94.4 us
    unnamed x16, local copies, waits for them, and re-layouts  2.91 us
    convert_element_type x2, other arithmetic, body(): t.astype(F32)  2.67 us

profile of v4, /device:TPU:1, one launch (start us, length us, event | category | flops | bytes accessed | tf_op | source)
XLA Modules:
  0.0 102.3 jit_solution(7332249743607482200)
XLA Ops:
  0.6 94.4 %layer.1 = (bf16[256,1024]{1,0:T(8,128)(2,1)}, bf16[256,1024]{1,0:T(8,128)(2,1)}, bf16[1024,128]{1,0:T(8,128)(2,1)}, bf16[1024,128]{1,0:T(8,128)(2,1)}, bf16[128...) custom-call(bf16[1024]{0:T(1024)(128)(2,1)} %gain_ref.1, s32[16,1024]{1,0:T(8,128)} %fin_ref.1, s32[16,1024]{1,0:T(8,128)} %fout_ref.1, ...), custom_call_target="tpu_custom_call" | custom-call | tf_op jit(solution)/shard_map/layer/pallas_call | solution.py:723
  95.0 0.0 copy-start
  95.0 0.0 copy-start.6
  95.0 1.8 %convert_element_type.18 = f32[1024,128]{1,0:T(8,128)} convert(bf16[1024,128]{1,0:T(8,128)(2,1)} %get-tuple-element.14) | non-fusion elementwise | flops 131072 | bytes 786432 | tf_op jit(solution)/shard_map/convert_element_type | solution.py:769
  96.9 0.0 copy-done
  96.9 0.0 copy-done.6
  96.9 0.0 copy-start.4
  96.9 0.8 convert_multiply_fusion.1
  97.7 0.1 copy-done.4
  97.8 0.0 copy-start.1
  97.8 0.0 copy-start.5
  97.8 0.8 convert_element_type.21
  98.7 0.1 copy-done.1
  98.8 0.2 copy-done.5
  99.1 0.0 copy-start.3
  99.1 0.9 convert_multiply_fusion
  99.9 0.4 copy-done.3
  100.3 0.0 copy-start.2
  100.3 0.8 copy.24
  101.1 0.4 copy-done.2
  101.5 0.8 copy.25
Async XLA Ops:
  95.0 1.9 %copy-start = (bf16[1024,128]{1,0:T(8,128)(2,1)S(1)}, bf16[1024,128]{1,0:T(8,128)(2,1)}, u32[]{:S(2)}) copy-start(bf16[1024,128]{1,0:T(8,128)(2,1)} %refs_2_.1) | copy-start | bytes 786436
  95.0 1.8 %copy-start.6 = (bf16[1024,128]{1,0:T(8,128)(2,1)S(1)}, bf16[1024,128]{1,0:T(8,128)(2,1)}, u32[]{:S(2)}) copy-start(bf16[1024,128]{1,0:T(8,128)(2,1)} %get-tuple-element.15) | copy-start | bytes 786436
  96.9 1.0 copy-start.4
  97.8 1.0 copy-start.1
  97.8 1.2 %copy-start.5 = (bf16[128,1024]{1,0:T(8,128)(2,1)S(1)}, bf16[128,1024]{1,0:T(8,128)(2,1)}, u32[]{:S(2)}) copy-start(bf16[128,1024]{1,0:T(8,128)(2,1)} %get-tuple-element.17) | copy-start | bytes 786436
  99.1 1.2 %copy-start.3 = (bf16[256,1024]{1,0:T(8,128)(2,1)S(1)}, bf16[256,1024]{1,0:T(8,128)(2,1)}, u32[]{:S(2)}) copy-start(bf16[256,1024]{1,0:T(8,128)(2,1)} %get-tuple-element.12) | copy-start | bytes 1572868
  100.3 1.2 %copy-start.2 = (bf16[256,1024]{1,0:T(8,128)(2,1)S(1)}, bf16[256,1024]{1,0:T(8,128)(2,1)}, u32[]{:S(2)}) copy-start(bf16[256,1024]{1,0:T(8,128)(2,1)} %get-tuple-element.13) | copy-start | bytes 1572868
